TPU v7x, 32 devices: a whole 2x2x4 slice. The times are simulated.
32 devices in a mesh: rep: 2 (over x), kv: 16 (over z, y, core).
Axes of the slice: x: 2, y: 2, z: 4, core: 2. Of those that a mesh axis runs over, the one named last changes fastest.
Arguments:
- queries: bfloat16 [32, 3, 36864], P('rep', None, 'kv'), parts along dimension 0, may hold values from -4 to 4
- cache: bfloat16 [8192, 16, 576], P(('rep', 'kv')), parts along dimension 0, may hold values from -4 to 4
- page_counts: int32 [32], P('rep'), parts along dimension 0, may hold values from 1 to 2048, as said below
- slot_request: int32 [1024], P(('rep', 'kv')), parts along dimension 0, may hold values from 0 to 15, as said below
- slot_start: int32 [1024], P(('rep', 'kv')), parts along dimension 0, may hold values from 0 to 2040, as said below
- slot_live: int32 [1024], P(('rep', 'kv')), parts along dimension 0, may hold values from 1 to 8, as said below
- slot_pages: int32 [1024, 8], P(('rep', 'kv')), parts along dimension 0, may hold values from 0 to 255, as said below
Outputs:
- attended: bfloat16 [32, 3, 32768], P('rep', None, 'kv'), parts along dimension 0
- lse: float32 [32, 3, 64], P('rep'), parts along dimension 0
There are 2 independent parts, one for each index of `rep`. A program takes and returns all parts, laid end to end along the dimension named above; each array names one. Nothing has to cross between parts.
Inputs may be any that keep to these rules, and one draw needn't show every extreme that they name: Request r has 16 * page_counts[r] tokens; the slots that name r cover its pages 0 to page_counts[r] - 1, each exactly once; one request holds 8 * (256) pages. `slot_request`: every request is named by at least one slot; slot s lives on index s // 32 of kv. Slot s covers pages slot_start[s] to slot_start[s] + slot_live[s] - 1 of its request. Only the first slot_live[s] entries of slot_pages[s] are used. `slot_pages`: page numbers local to the device that holds the slot; all entries of one device's slots are distinct.
All inputs are finite; a program needn't handle non-finite values.
Results may differ from a plain program's by a relative error of at most 0.0043.
Values may be sent and summed in bfloat16 or wider, within the bound.
A program may use at most 128 MiB of HBM per device.

v0:
```python
import jax
import jax.numpy as jnp
from jax import lax
from jax.sharding import PartitionSpec as P

ROPE = 64


softmax_scale = 192.0 ** (-0.5)
neg_floor = -1e30
block_slots = 8


def slot_partials(
    query_heads, key_rows, request, first_page, live_pages, page_counts, page_rows, latent
):
    row_count = key_rows.shape[1]
    query_count = query_heads.shape[1]
    request_count = page_counts.shape[0]
    chosen = query_heads[request]
    scores = (
        jnp.einsum("gqhc,gjc->gqhj", chosen, key_rows, preferred_element_type=jnp.float32)
        * softmax_scale
    )
    row_ids = jnp.arange(row_count, dtype=jnp.int32)
    page_of = row_ids // page_rows
    position = (first_page[:, None] + page_of[None, :]) * page_rows + row_ids[None, :] % page_rows
    member = request[:, None] == jnp.arange(request_count, dtype=jnp.int32)[None, :]
    request_pages = jnp.sum(jnp.where(member, page_counts[None, :], 0), axis=1)
    query_ids = jnp.arange(query_count, dtype=jnp.int32)
    limit = request_pages[:, None] * page_rows - (query_count - 1 - query_ids)[None, :]
    visible = (page_of[None, None, :] < live_pages[:, None, None]) & (
        position[:, None, :] < limit[:, :, None]
    )
    visible = visible[:, :, None, :]
    slot_max = jnp.max(jnp.where(visible, scores, neg_floor), axis=3)
    shifted = jnp.where(visible, scores - slot_max[..., None], neg_floor)
    weights = jnp.exp(shifted)
    slot_sum = jnp.sum(weights, axis=3)
    rounded = weights.astype(jnp.bfloat16)
    slot_out = jnp.einsum(
        "gqhj,gjc->gqhc", rounded, key_rows[:, :, :latent], preferred_element_type=jnp.float32
    )
    return (slot_max, slot_sum, slot_out)


def fold_slots(carry, request, slot_max, slot_sum, slot_out):
    best, denom, numer = carry
    request_count = best.shape[0]
    member = request[:, None] == jnp.arange(request_count, dtype=jnp.int32)[None, :]
    block_best = jnp.max(jnp.where(member[:, :, None, None], slot_max[:, None], neg_floor), axis=0)
    new_best = jnp.maximum(best, block_best)
    kept = jnp.exp(best - new_best)
    member_float = member.astype(jnp.float32)
    slot_best = jnp.einsum("gr,rqh->gqh", member_float, new_best, precision=lax.Precision.HIGHEST)
    factor = jnp.exp(slot_max - slot_best)
    denom = denom * kept + jnp.einsum(
        "gr,gqh->rqh", member_float, factor * slot_sum, precision=lax.Precision.HIGHEST
    )
    numer = numer * kept[..., None] + jnp.einsum(
        "gr,gqhc->rqhc", member_float, factor[..., None] * slot_out, precision=lax.Precision.HIGHEST
    )
    return (new_best, denom, numer)


def per_device(queries, cache, page_counts, slot_request, slot_start, slot_live, slot_pages):
    gathered = lax.all_gather(queries, "kv", axis=2, tiled=True)
    request_count, query_count, flat_width = gathered.shape
    token_width = cache.shape[2]
    head_count = flat_width // token_width
    latent = token_width - ROPE
    page_rows = cache.shape[1]
    query_heads = gathered.reshape(request_count, query_count, head_count, token_width)
    local_slots = slot_request.shape[0]
    slot_span = slot_pages.shape[1]
    block_count = local_slots // block_slots

    def one_block(carry, block_index):
        first_slot = block_index * block_slots

        def pick_rows(source):
            return lax.dynamic_slice_in_dim(source, first_slot, block_slots, 0)

        request = pick_rows(slot_request)
        first_page = pick_rows(slot_start)
        live_pages = pick_rows(slot_live)
        pages = pick_rows(slot_pages)
        key_rows = cache[pages.reshape(-1)].reshape(block_slots, slot_span * page_rows, token_width)
        slot_max, slot_sum, slot_out = slot_partials(
            query_heads, key_rows, request, first_page, live_pages, page_counts, page_rows, latent
        )
        return (fold_slots(carry, request, slot_max, slot_sum, slot_out), None)

    initial = (
        jnp.full((request_count, query_count, head_count), neg_floor, jnp.float32),
        jnp.zeros((request_count, query_count, head_count), jnp.float32),
        jnp.zeros((request_count, query_count, head_count, latent), jnp.float32),
    )
    (best, denom, numer), _unused = lax.scan(
        one_block, initial, jnp.arange(block_count, dtype=jnp.int32)
    )
    partial_value = numer.astype(jnp.bfloat16)
    device_count = lax.axis_size("kv")
    columns = head_count * latent // device_count
    first_column = lax.axis_index("kv") * columns
    local_head_count = max(1, columns // latent)
    repeat_count = min(columns, latent)
    first_head = first_column // latent
    highest = lax.pmax(best, "kv")
    shrink = jnp.exp(best - highest)
    widened = lax.optimization_barrier(partial_value).astype(jnp.float32)
    scaled = (widened * shrink[..., None]).reshape(request_count, query_count, head_count * latent)
    summed = lax.psum_scatter(scaled, "kv", scatter_dimension=2, tiled=True)
    total = lax.psum(denom * shrink, "kv")
    last_axis = total.ndim - 1
    picked = lax.dynamic_slice_in_dim(total, first_head, local_head_count, last_axis)
    attended = (summed / jnp.repeat(picked, repeat_count, axis=last_axis)).astype(jnp.bfloat16)
    lse = highest + jnp.log(total)
    return (attended, lse)


def solution(mesh):
    in_specs = (
        P("rep", None, "kv"),
        P(("rep", "kv"), None, None),
        P("rep"),
        P(("rep", "kv")),
        P(("rep", "kv")),
        P(("rep", "kv")),
        P(("rep", "kv"), None),
    )
    out_specs = (P("rep", None, "kv"), P("rep", None, None))
    return jax.shard_map(
        per_device, mesh=mesh, in_specs=in_specs, out_specs=out_specs, check_vma=False
    )
```

profile of v0, /device:TPU:0, one launch (start us, length us, event | category | flops | bytes accessed | tf_op | source)
XLA Modules:
  0.0 312.5 jit_solution(14193493262367248329)
XLA Ops:
  8.0 8.9 %copy.46 = bf16[256,16,576]{2,1,0:T(8,128)(2,1)} copy(bf16[256,16,576]{0,2,1:T(8,128)(2,1)} %param.10) | data formatting | bytes 9437184
  16.9 43.7 %all-gather.2.cloned.1.call-done = bf16[16,3,36864]{2,0,1:T(8,128)(2,1)} async-done(((bf16[16,3,2304]{2,0,1:T(8,128)(2,1)}), bf16[16,3,36864]{2,0,1:T(8,128)(2,1)}) %all-gather.2.cloned.1.call-update) | async-done | bytes 3538960 | tf_op jit(solution)/shard_map/all_gather | solution.py:67
  60.6 7.7 %reshape.235 = bf16[16,3,64,576]{3,2,0,1:T(8,128)(2,1)} reshape(bf16[16,3,36864]{2,0,1:T(8,128)(2,1)} %all-gather.2.cloned.1.call-done) | data formatting | bytes 7077888 | tf_op jit(solution)/shard_map/reshape | solution.py:73
  68.4 4.5 %copy.44 = bf16[16,3,64,576]{3,2,1,0:T(8,128)(2,1)} copy(bf16[16,3,64,576]{3,2,0,1:T(8,128)(2,1)} %reshape.235) | data formatting | bytes 7077888
  72.9 81.9 %while.17 = (s32[]{:T(128)}, f32[16,3,64]{2,0,1:T(8,128)S(1)}, f32[16,3,64]{2,0,1:T(8,128)S(1)}, f32[16,3,64,512]{3,0,2,1:T(8,128)}, s32[4]{0:T(128)S(1)}, /*ind...) while((s32[]{:T(128)}, f32[16,3,64]{2,0,1:T(8,128)S(1)}, ...), condition=%wide.region_5.6_spmd.clone, body=%wide.region_0.5_spmd.clone.sunk | while | flops 586757760 | bytes 34555300 | solution.py:99
  74.9 3.0 gather_fusion
  78.2 3.3 %gather_fusion.1 = bf16[64,16,576]{2,1,0:T(8,128)(2,1)S(1)} fusion(bf16[256,16,576]{2,1,0:T(8,128)(2,1)} %get-tuple-element.412, s32[1024]{0:T(1024)S(1)} %pad_clamp_fusion.5), kind=kCustom, calls=%fused_computation.1.clone.clone.1 | custom fusion | bytes 2359552 | tf_op jit(solution)/shard_map/while/body/eval_jaxpr/gather | solution.py:88
  85.9 5.7 %fusion.47 = f32[16,3,64,512]{3,0,2,1:T(8,128)} fusion(f32[16,3,64,512]{3,0,2,1:T(8,128)} %get-tuple-element.388, f32[16,3,64]{0,2,1:T(8,128)S(1)} %copy.73, pred[]{:T(512)S(6)} %compare.12, f32[8,3,64,512]{3,2,1,0:T(8,128)S(1)} %convolution_multiply_fusion.3, s32[8]{0:T(128)S(1)} %get-tuple-element.361), kind=kOutput, calls=%fused_computation.3.clone.1 | convolution fusion | flops 155713664 | bytes 15740961 | tf_op jit(solution)/shard_map/while/body/eval_jaxpr/gr,gqhc->rqhc/dot_general | solution.py:60
  93.5 3.0 gather_fusion
  96.8 3.3 %gather_fusion.1 = bf16[64,16,576]{2,1,0:T(8,128)(2,1)S(1)} fusion(bf16[256,16,576]{2,1,0:T(8,128)(2,1)} %get-tuple-element.412, s32[1024]{0:T(1024)S(1)} %pad_clamp_fusion.5), kind=kCustom, calls=%fused_computation.1.clone.clone.1 | custom fusion | bytes 2359552 | tf_op jit(solution)/shard_map/while/body/eval_jaxpr/gather | solution.py:88
  104.5 8.1 %fusion.47 = f32[16,3,64,512]{3,0,2,1:T(8,128)} fusion(f32[16,3,64,512]{3,0,2,1:T(8,128)} %get-tuple-element.388, f32[16,3,64]{0,2,1:T(8,128)S(1)} %copy.73, pred[]{:T(512)S(6)} %compare.12, f32[8,3,64,512]{3,2,1,0:T(8,128)S(1)} %convolution_multiply_fusion.3, s32[8]{0:T(128)S(1)} %get-tuple-element.361), kind=kOutput, calls=%fused_computation.3.clone.1 | convolution fusion | flops 155713664 | bytes 15740961 | tf_op jit(solution)/shard_map/while/body/eval_jaxpr/gr,gqhc->rqhc/dot_general | solution.py:60
  114.6 3.0 gather_fusion
  117.9 3.3 %gather_fusion.1 = bf16[64,16,576]{2,1,0:T(8,128)(2,1)S(1)} fusion(bf16[256,16,576]{2,1,0:T(8,128)(2,1)} %get-tuple-element.412, s32[1024]{0:T(1024)S(1)} %pad_clamp_fusion.5), kind=kCustom, calls=%fused_computation.1.clone.clone.1 | custom fusion | bytes 2359552 | tf_op jit(solution)/shard_map/while/body/eval_jaxpr/gather | solution.py:88
  123.8 1.8 convolution_multiply_fusion.3
  125.5 8.1 %fusion.47 = f32[16,3,64,512]{3,0,2,1:T(8,128)} fusion(f32[16,3,64,512]{3,0,2,1:T(8,128)} %get-tuple-element.388, f32[16,3,64]{0,2,1:T(8,128)S(1)} %copy.73, pred[]{:T(512)S(6)} %compare.12, f32[8,3,64,512]{3,2,1,0:T(8,128)S(1)} %convolution_multiply_fusion.3, s32[8]{0:T(128)S(1)} %get-tuple-element.361), kind=kOutput, calls=%fused_computation.3.clone.1 | convolution fusion | flops 155713664 | bytes 15740961 | tf_op jit(solution)/shard_map/while/body/eval_jaxpr/gr,gqhc->rqhc/dot_general | solution.py:60
  135.7 3.0 gather_fusion
  138.9 3.3 %gather_fusion.1 = bf16[64,16,576]{2,1,0:T(8,128)(2,1)S(1)} fusion(bf16[256,16,576]{2,1,0:T(8,128)(2,1)} %get-tuple-element.412, s32[1024]{0:T(1024)S(1)} %pad_clamp_fusion.5), kind=kCustom, calls=%fused_computation.1.clone.clone.1 | custom fusion | bytes 2359552 | tf_op jit(solution)/shard_map/while/body/eval_jaxpr/gather | solution.py:88
  144.8 1.8 convolution_multiply_fusion.3
  146.6 8.1 %fusion.47 = f32[16,3,64,512]{3,0,2,1:T(8,128)} fusion(f32[16,3,64,512]{3,0,2,1:T(8,128)} %get-tuple-element.388, f32[16,3,64]{0,2,1:T(8,128)S(1)} %copy.73, pred[]{:T(512)S(6)} %compare.12, f32[8,3,64,512]{3,2,1,0:T(8,128)S(1)} %convolution_multiply_fusion.3, s32[8]{0:T(128)S(1)} %get-tuple-element.361), kind=kOutput, calls=%fused_computation.3.clone.1 | convolution fusion | flops 155713664 | bytes 15740961 | tf_op jit(solution)/shard_map/while/body/eval_jaxpr/gr,gqhc->rqhc/dot_general | solution.py:60
  154.8 3.3 %convert_element_type.16 = bf16[16,3,64,512]{3,0,2,1:T(8,128)(2,1)S(1)} convert(f32[16,3,64,512]{3,0,2,1:T(8,128)} %get-tuple-element.156) | non-fusion elementwise | flops 1572864 | bytes 9437184 | tf_op jit(solution)/shard_map/convert_element_type | solution.py:102
  158.0 59.0 %pmax.7 = f32[16,3,64]{2,0,1:T(8,128)S(1)} all-reduce(f32[16,3,64]{2,0,1:T(8,128)S(1)} %get-tuple-element.157), channel_id=1, replica_groups=mesh['rep'=2,'kv'=16] {'kv'}, use_global_device_ids=true, to_apply=%region_6.7 | all-reduce | flops 3072 | bytes 24576 | tf_op jit(solution)/shard_map/pmax | solution.py:109
  217.6 3.4 %copy.55 = f32[3,64,2,8,512]{4,3,1,2,0:T(8,128)} copy(f32[3,64,2,8,512]{4,3,2,1,0:T(8,128)S(1)} %multiply_bitcast_fusion) | data formatting | bytes 12582912 | tf_op jit(solution)/shard_map/reshape | solution.py:112
  221.0 59.3 %psum.7 = f32[16,3,64]{2,0,1:T(8,128)S(1)} all-reduce(f32[16,3,64]{2,0,1:T(8,128)S(1)} %get-tuple-element.274), channel_id=1, replica_groups=mesh['rep'=2,'kv'=16] {'kv'}, use_global_device_ids=true, to_apply=%region_8.9 | all-reduce | flops 3072 | bytes 24576 | tf_op jit(solution)/shard_map/psum | solution.py:114
  281.4 22.5 %reduce-scatter.2.cloned.1.call-done = f32[16,3,2048]{2,0,1:T(8,128)} async-done(((f32[16,3,32768]{2,0,1:T(8,128)}), f32[16,3,2048]{2,0,1:T(8,128)}) %reduce-scatter.2.cloned.1.call-update) | async-done | bytes 393232 | tf_op jit(solution)/shard_map/reduce_scatter | solution.py:113
  (144 shorter events, 24.3 us)
Async XLA Ops:
  7.2 53.4 %all-gather.2.cloned.1.call-start = ((), (), s32[]{:S(2)}) async-start(), calls=%async_computation.1 | async-start | bytes 3760128 | tf_op jit(solution)/shard_map/all_gather | solution.py:67
  7.9 296.0 %reduce-scatter.2.cloned.1.call-start = ((), (), s32[]{:S(2)}) async-start(), calls=%async_computation.2 | async-start | bytes 6684672 | tf_op jit(solution)/shard_map/reduce_scatter | solution.py:113
  68.3 4.5 %copy-start.1 = (s32[32,8]{0,1:T(8,128)S(1)}, s32[32,8]{0,1:T(8,128)}, u32[]{:S(2)}) copy-start(s32[32,8]{0,1:T(8,128)} %param.15) | copy-start | bytes 3076
  68.3 4.5 %copy-start.2 = (s32[32]{0:T(128)S(1)}, s32[32]{0:T(128)}, u32[]{:S(2)}) copy-start(s32[32]{0:T(128)} %param.12) | copy-start | bytes 388
  68.3 4.5 %copy-start.3 = (s32[32]{0:T(128)S(1)}, s32[32]{0:T(128)}, u32[]{:S(2)}) copy-start(s32[32]{0:T(128)} %param.14) | copy-start | bytes 388
  68.3 4.5 %copy-start.4 = (s32[32]{0:T(128)S(1)}, s32[32]{0:T(128)}, u32[]{:S(2)}) copy-start(s32[32]{0:T(128)} %param.13) | copy-start | bytes 388
  68.4 4.5 %copy-start.5 = (s32[16]{0:T(128)S(1)}, s32[16]{0:T(128)}, u32[]{:S(2)}) copy-start(s32[16]{0:T(128)} %param.11) | copy-start | bytes 196
  82.3 0.9 copy-start
  100.9 0.9 copy-start
  121.9 0.9 copy-start
  143.0 0.9 copy-start
Sparse Core Ops, SparseCore 0:
  10.3 50.2 all-gather.1
  221.1 82.7 reduce-scatter.1
where the time goes:
time: 314 us; the launch traced here: 313 us
  blocking collectives  118 us (38%)
  waiting for transfers between devices  66.9 us (21%)
  local copies, waits for them, and re-layouts  56.5 us (18%)
  matrix products  42.2 us (13%)
  between operations  14.2 us (5%)
  other arithmetic  11.4 us (4%)
    psum x1, blocking collectives, per_device(): total = lax.psum(denom * shrink, 'kv')  59.3 us
    pmax x1, blocking collectives, per_device(): highest = lax.pmax(best, 'kv')  59 us
    all_gather x1, waiting for transfers between devices, per_device(): gathered = lax.all_gather(queries, 'kv', axis=2, tiled=True)  43.7 us
    dot_general x4, matrix products, fold_slots(): jnp.einsum('gr,gqhc->rqhc', member_float, factor[..., None] * slot_out, p...  30 us
    reduce_scatter x1, waiting for transfers between devices, per_device(): summed = lax.psum_scatter(scaled, 'kv', scatter_dimension=2, tiled=True)  22.5 us
    unnamed x12, local copies, waits for them, and re-layouts  13.4 us
    gather x4, local copies, waits for them, and re-layouts, one_block(): cache[pages.reshape(-1)]  13.1 us
    gather x4, local copies, waits for them, and re-layouts, slot_partials(): chosen = query_heads[request]  12.1 us
  transfers between devices with their start and end apart: 2, of which 2 were waited for; matrix products, arithmetic and copies ran while one was open for 3% of the time, Pallas kernels for 0%

commit v1 on v0

v1 whole, which is shorter than its diff:
```python
import functools

import jax
import jax.numpy as jnp
from jax import lax
from jax.experimental import pallas as pl
from jax.experimental.pallas import tpu as pltpu
from jax.sharding import PartitionSpec as P

ROPE = 64
CORES = 2
LANES = 128
softmax_scale = 192.0 ** (-0.5)
neg_floor = -1e30
slot_group = 4
vmem_limit = 56 * 1024 * 1024


def place(chip_rows):
    index = lax.axis_index("kv")
    z = index // (2 * CORES)
    y = (index // CORES) % 2
    core = index % CORES
    return index, z, y, core


def device_of(z, y, core):
    return (z * 2 + y) * CORES + core


def gather_kernel(rows_z, x_ref, o_ref, local_sem, send_sems, recv_sems):
    index, z, y, core = place(rows_z)
    other_y, other_core = 1 - y, 1 - core
    has_up, has_down = z < rows_z - 1, z > 0
    barrier = pltpu.get_barrier_semaphore()

    def greet(target):
        pl.semaphore_signal(barrier, inc=1, device_id={"kv": target})

    pl.when(has_up)(lambda: greet(device_of(z + 1, y, core)))
    pl.when(has_down)(lambda: greet(device_of(z - 1, y, core)))
    greet(device_of(z, other_y, core))
    greet(device_of(z, y, other_core))
    pl.semaphore_wait(barrier, 2 + has_up.astype(jnp.int32) + has_down.astype(jnp.int32))

    def copy(slot, way, source=None):
        target = (
            device_of(jnp.minimum(z + 1, rows_z - 1), y, core),
            device_of(jnp.maximum(z - 1, 0), y, core),
            device_of(z, other_y, core),
            device_of(z, y, other_core),
        )[way]
        return pltpu.make_async_remote_copy(
            src_ref=o_ref.at[slot] if source is None else source,
            dst_ref=o_ref.at[slot],
            send_sem=send_sems.at[slot, way],
            recv_sem=recv_sems.at[slot],
            device_id={"kv": target},
        )

    own = pltpu.make_async_copy(x_ref, o_ref.at[index], local_sem)
    own.start()
    pl.when(has_up)(lambda: copy(index, 0, x_ref).start())
    pl.when(has_down)(lambda: copy(index, 1, x_ref).start())
    copy(index, 2, x_ref).start()
    copy(index, 3, x_ref).start()

    def from_below(step):
        slot = device_of(z - step, y, core)
        copy(slot, 3).wait_recv()
        pl.when(has_up)(lambda: copy(slot, 0).start())
        copy(slot, 2).start()
        copy(slot, 3).start()

    def from_above(step):
        slot = device_of(z + step, y, core)
        copy(slot, 3).wait_recv()
        pl.when(has_down)(lambda: copy(slot, 1).start())
        copy(slot, 2).start()
        copy(slot, 3).start()

    def across(row):
        slot = device_of(row, other_y, core)
        copy(slot, 3).wait_recv()
        copy(slot, 3).start()

    def across_pair(step):
        if step == 0:
            across(z)
        else:
            pl.when(z >= step)(lambda: across(z - step))
            pl.when(z + step < rows_z)(lambda: across(z + step))

    for step in range(1, rows_z):
        pl.when(z >= step)(functools.partial(from_below, step))
        pl.when(z + step < rows_z)(functools.partial(from_above, step))
        across_pair(step - 1)
    across_pair(rows_z - 1)
    for row in range(rows_z):
        for column in range(2):
            copy(device_of(row, column, other_core), 3).wait_recv()

    own.wait()
    for row in range(rows_z):
        slot = device_of(row, y, core)
        pl.when(has_up & (row <= z))(lambda slot=slot: copy(slot, 0).wait_send())
        pl.when(has_down & (row >= z))(lambda slot=slot: copy(slot, 1).wait_send())
        copy(slot, 2).wait_send()
        copy(slot, 3).wait_send()
        copy(device_of(row, other_y, core), 3).wait_send()


def gather_queries(shard, rows_z):
    count = rows_z * 2 * CORES
    return pl.pallas_call(
        functools.partial(gather_kernel, rows_z),
        out_shape=jax.ShapeDtypeStruct((count,) + shard.shape, shard.dtype),
        in_specs=[pl.BlockSpec(memory_space=pl.ANY)],
        out_specs=pl.BlockSpec(memory_space=pl.ANY),
        scratch_shapes=[
            pltpu.SemaphoreType.DMA,
            pltpu.SemaphoreType.DMA((count, 4)),
            pltpu.SemaphoreType.DMA((count,)),
        ],
        compiler_params=pltpu.CompilerParams(collective_id=0, has_side_effects=True),
        name="gather_queries",
    )(shard)


def attend_kernel(
    latent, query_count, counts, request, start, live, pages, q_ref, cache_ref, numer_ref, best_ref,
    denom_ref
):
    slots, span = pages.shape
    page_rows = cache_ref.shape[1]
    rows = q_ref.shape[1]
    heads = rows // query_count
    keys = span * page_rows
    best_ref[...] = jnp.full(best_ref.shape, neg_floor, jnp.float32)
    denom_ref[...] = jnp.zeros(denom_ref.shape, jnp.float32)
    numer_ref[...] = jnp.zeros(numer_ref.shape, jnp.float32)
    key_ids = lax.broadcasted_iota(jnp.int32, (rows, keys), 1)
    query_ids = lax.broadcasted_iota(jnp.int32, (rows, keys), 0) // heads

    def group(block, carry):
        parts = []
        for offset in range(slot_group):
            slot = block * slot_group + offset
            r = request[slot]
            key_rows = jnp.concatenate([cache_ref[pages[slot, k]] for k in range(span)], axis=0)
            scores = (
                lax.dot_general(
                    q_ref[r], key_rows, (((1,), (1,)), ((), ())),
                    preferred_element_type=jnp.float32,
                )
                * softmax_scale
            )
            bound = (counts[r] - start[slot]) * page_rows - (query_count - 1)
            visible = (key_ids < live[slot] * page_rows) & (key_ids - query_ids < bound)
            top = jnp.max(jnp.where(visible, scores, neg_floor), axis=1, keepdims=True)
            weights = jnp.where(visible, jnp.exp(scores - top), 0.0)
            total = jnp.sum(weights, axis=1, keepdims=True)
            out = jnp.dot(
                weights.astype(jnp.bfloat16), key_rows[:, :latent],
                preferred_element_type=jnp.float32,
            )
            parts.append((r, top, total, out))
        for r, top, total, out in parts:
            old = best_ref[r]
            new = jnp.maximum(old, top)
            kept = jnp.exp(old - new)
            factor = jnp.exp(top - new)
            best_ref[r] = new
            denom_ref[r] = denom_ref[r] * kept + factor * total
            for first in range(0, latent, LANES):
                columns = slice(first, first + LANES)
                numer_ref[r, :, columns] = (
                    numer_ref[r, :, columns] * kept + out[:, columns] * factor
                )
        return carry

    lax.fori_loop(0, slots // slot_group, group, 0)


def attend(queries, cache, counts, request, start, live, pages, latent, query_count):
    requests, rows, _width = queries.shape
    smem = pl.BlockSpec(memory_space=pltpu.SMEM)
    vmem = pl.BlockSpec(memory_space=pltpu.VMEM)
    return pl.pallas_call(
        functools.partial(attend_kernel, latent, query_count),
        out_shape=(
            jax.ShapeDtypeStruct((requests, rows, latent), jnp.float32),
            jax.ShapeDtypeStruct((requests, rows, LANES), jnp.float32),
            jax.ShapeDtypeStruct((requests, rows, LANES), jnp.float32),
        ),
        in_specs=[smem] * 5 + [vmem] * 2,
        out_specs=(vmem, vmem, vmem),
        compiler_params=pltpu.CompilerParams(vmem_limit_bytes=vmem_limit),
        name="attend",
    )(counts, request, start, live, pages, queries, cache)


def stats_kernel(rows_z, in_ref, out_ref, core_buf, y_buf, z_buf, core_sems, y_sems, z_sems, z_recv):
    index, z, y, core = place(rows_z)
    barrier = pltpu.get_barrier_semaphore()
    others = [device_of(z, y, 1 - core), device_of(z, 1 - y, core)]
    others += [device_of((z + step) % rows_z, y, core) for step in range(1, rows_z)]
    for target in others:
        pl.semaphore_signal(barrier, inc=1, device_id={"kv": target})
    pl.semaphore_wait(barrier, len(others))

    def combine(buf, count):
        top = buf[0, 0]
        for item in range(1, count):
            top = jnp.maximum(top, buf[item, 0])
        total = buf[0, 1] * jnp.exp(buf[0, 0] - top)
        for item in range(1, count):
            total = total + buf[item, 1] * jnp.exp(buf[item, 0] - top)
        return top, total

    def swap(buf, sems, me, target):
        copy = pltpu.make_async_remote_copy(
            src_ref=buf.at[me], dst_ref=buf.at[me], send_sem=sems.at[0], recv_sem=sems.at[1],
            device_id={"kv": target},
        )
        copy.start()
        copy.wait()

    core_buf[core] = in_ref[...]
    swap(core_buf, core_sems, core, others[0])
    top, total = combine(core_buf, CORES)
    y_buf[y, 0] = top
    y_buf[y, 1] = total
    swap(y_buf, y_sems, y, others[1])
    top, total = combine(y_buf, 2)
    z_buf[z, 0] = top
    z_buf[z, 1] = total

    def z_copy(step, source):
        return pltpu.make_async_remote_copy(
            src_ref=z_buf.at[source], dst_ref=z_buf.at[source], send_sem=z_sems.at[step],
            recv_sem=z_recv.at[source], device_id={"kv": device_of((z + step) % rows_z, y, core)},
        )

    for step in range(1, rows_z):
        z_copy(step, z).start()
    for step in range(1, rows_z):
        z_copy(step, (z + step) % rows_z).wait_recv()
    for step in range(1, rows_z):
        z_copy(step, z).wait_send()
    top, total = combine(z_buf, rows_z)
    out_ref[0] = top
    out_ref[1] = total


def combine_stats(stats, rows_z):
    vmem = pl.BlockSpec(memory_space=pltpu.VMEM)
    return pl.pallas_call(
        functools.partial(stats_kernel, rows_z),
        out_shape=jax.ShapeDtypeStruct(stats.shape, stats.dtype),
        in_specs=[vmem],
        out_specs=vmem,
        scratch_shapes=[
            pltpu.VMEM((CORES,) + stats.shape, stats.dtype),
            pltpu.VMEM((2,) + stats.shape, stats.dtype),
            pltpu.VMEM((rows_z,) + stats.shape, stats.dtype),
            pltpu.SemaphoreType.DMA((2,)),
            pltpu.SemaphoreType.DMA((2,)),
            pltpu.SemaphoreType.DMA((rows_z,)),
            pltpu.SemaphoreType.DMA((rows_z,)),
        ],
        compiler_params=pltpu.CompilerParams(collective_id=1, has_side_effects=True),
        name="combine_stats",
    )(stats)


def reduce_kernel(
    rows_z, x_ref, out_ref, core_in, y_out, y_in, z_out, z_in, core_send, core_recv, y_send, y_recv,
    z_send, z_recv
):
    index, z, y, core = place(rows_z)
    other_y, other_core = 1 - y, 1 - core
    partner, across = device_of(z, y, other_core), device_of(z, other_y, core)
    barrier = pltpu.get_barrier_semaphore()
    others = [partner, across]
    others += [device_of((z + step) % rows_z, y, core) for step in range(1, rows_z)]
    for target in others:
        pl.semaphore_signal(barrier, inc=1, device_id={"kv": target})
    pl.semaphore_wait(barrier, len(others))

    def row_of(step):
        return (z + step) % rows_z

    steps = list(range(1, rows_z)) + [0]

    def core_copy(side, step):
        column = other_y if side == 0 else y
        return pltpu.make_async_remote_copy(
            src_ref=x_ref.at[device_of(row_of(step), column, other_core)],
            dst_ref=core_in.at[side, step],
            send_sem=core_send.at[side, step],
            recv_sem=core_recv.at[side, step],
            device_id={"kv": partner},
        )

    def y_copy(step):
        return pltpu.make_async_remote_copy(
            src_ref=y_out.at[step], dst_ref=y_in.at[step], send_sem=y_send.at[step],
            recv_sem=y_recv.at[step], device_id={"kv": across},
        )

    def z_copy(step):
        return pltpu.make_async_remote_copy(
            src_ref=z_out.at[step], dst_ref=z_in.at[step], send_sem=z_send.at[step],
            recv_sem=z_recv.at[step],
            device_id={"kv": device_of(row_of(step), y, core)},
        )

    for side in range(2):
        for step in steps:
            core_copy(side, step).start()

    def wide(value):
        return value.astype(jnp.float32)

    for step in steps:
        core_copy(0, step).wait_recv()
        mine = x_ref[device_of(row_of(step), other_y, core)]
        y_out[step] = (wide(mine) + wide(core_in[0, step])).astype(y_out.dtype)
        y_copy(step).start()
    for step in steps:
        core_copy(1, step).wait_recv()
        y_copy(step).wait_recv()
        mine = x_ref[device_of(row_of(step), y, core)]
        total = wide(mine) + wide(core_in[1, step]) + wide(y_in[step])
        if step:
            z_out[step] = total.astype(z_out.dtype)
            z_copy(step).start()
        else:
            out_ref[...] = total
    for step in range(1, rows_z):
        z_copy(step).wait_recv()
        out_ref[...] += wide(z_in[step])
    for step in steps:
        core_copy(0, step).wait_send()
        core_copy(1, step).wait_send()
        y_copy(step).wait_send()
        if step:
            z_copy(step).wait_send()


def reduce_partials(parts, rows_z):
    block = parts.shape[1:]
    vmem = pl.BlockSpec(memory_space=pltpu.VMEM)
    dma = pltpu.SemaphoreType.DMA
    return pl.pallas_call(
        functools.partial(reduce_kernel, rows_z),
        out_shape=jax.ShapeDtypeStruct(block, jnp.float32),
        in_specs=[vmem],
        out_specs=vmem,
        scratch_shapes=[
            pltpu.VMEM((2, rows_z) + block, parts.dtype),
            pltpu.VMEM((rows_z,) + block, parts.dtype),
            pltpu.VMEM((rows_z,) + block, parts.dtype),
            pltpu.VMEM((rows_z,) + block, parts.dtype),
            pltpu.VMEM((rows_z,) + block, parts.dtype),
            dma((2, rows_z)),
            dma((2, rows_z)),
            dma((rows_z,)),
            dma((rows_z,)),
            dma((rows_z,)),
            dma((rows_z,)),
        ],
        compiler_params=pltpu.CompilerParams(
            collective_id=2, has_side_effects=True, vmem_limit_bytes=vmem_limit
        ),
        name="reduce_partials",
    )(parts)


def per_device(queries, cache, page_counts, slot_request, slot_start, slot_live, slot_pages):
    count = lax.axis_size("kv")
    requests, query_count, shard_width = queries.shape
    token_width = cache.shape[2]
    latent = token_width - ROPE
    heads = count * shard_width // token_width
    rows = query_count * heads
    rows_z = count // (2 * CORES)
    direct = shard_width % token_width == 0 and rows_z * 2 * CORES == count
    if direct:
        local_heads = shard_width // token_width
        shard = queries.reshape(requests * query_count, shard_width)
        gathered = gather_queries(shard, rows_z)
        heads_first = gathered.reshape(count, requests, query_count, local_heads, token_width)
        query_heads = heads_first.transpose(1, 2, 0, 3, 4).reshape(requests, rows, token_width)
    else:
        gathered = lax.all_gather(queries, "kv", axis=2, tiled=True)
        query_heads = gathered.reshape(requests, rows, token_width)
    numer, best, denom = attend(
        query_heads, cache, page_counts, slot_request, slot_start, slot_live, slot_pages, latent,
        query_count,
    )
    best, denom = best[:, :, 0], denom[:, :, 0]
    if direct and best.size % LANES == 0:
        stats = jnp.stack([best.reshape(-1, LANES), denom.reshape(-1, LANES)])
        merged = combine_stats(stats, rows_z)
        highest, total = merged[0].reshape(requests, rows), merged[1].reshape(requests, rows)
    else:
        highest = lax.pmax(best, "kv")
        total = lax.psum(denom * jnp.exp(best - highest), "kv")
    scaled = numer * jnp.exp(best - highest)[..., None]
    lse = (highest + jnp.log(total)).reshape(requests, query_count, heads)
    total = total.reshape(requests, query_count, heads)
    if direct:
        width = local_heads * latent
        parts = scaled.astype(jnp.bfloat16).reshape(
            requests, query_count, count, local_heads * latent
        )
        parts = parts.transpose(2, 0, 1, 3).reshape(count, requests * query_count, width)
        summed = reduce_partials(parts, rows_z).reshape(requests, query_count, width)
    else:
        flat = lax.optimization_barrier(scaled.reshape(requests * query_count, heads * latent))
        width = heads * latent // count
        summed = lax.psum_scatter(flat, "kv", scatter_dimension=1, tiled=True)
        summed = summed.reshape(requests, query_count, width)
    first_head = lax.axis_index("kv") * width // latent
    picked_heads = max(1, width // latent)
    picked = lax.dynamic_slice_in_dim(total, first_head, picked_heads, 2)
    picked = jnp.repeat(picked, min(width, latent), axis=2)
    return ((summed / picked).astype(jnp.bfloat16), lse)


def solution(mesh):
    in_specs = (
        P("rep", None, "kv"),
        P(("rep", "kv"), None, None),
        P("rep"),
        P(("rep", "kv")),
        P(("rep", "kv")),
        P(("rep", "kv")),
        P(("rep", "kv"), None),
    )
    out_specs = (P("rep", None, "kv"), P("rep", None, None))
    return jax.shard_map(
        per_device, mesh=mesh, in_specs=in_specs, out_specs=out_specs, check_vma=False
    )
```

time: 314 us -> 150 us (0.48)
  blocking collectives: 118 us -> 0 us
  Pallas kernels: 0 us -> 90.9 us
  waiting for transfers between devices: 66.9 us -> 0 us
  matrix products: 42.2 us -> 0 us
  between operations: 14.2 us -> 0.76 us
  other arithmetic: 11.4 us -> 6.03 us
  local copies, waits for them, and re-layouts: 56.5 us -> 51.4 us
    pallas_call x0 -> x4, Pallas kernels: none -> 90.9 us  [the longest x1 30.6 us: gather_queries(): pl.pallas_call(functools.partial(gather_kernel, rows_z), out_shape=jax.Sh...]
    psum x1 -> x0, blocking collectives: 59.3 us -> none  [per_device(): total = lax.psum(denom * shrink, 'kv')]
    pmax x1 -> x0, blocking collectives: 59 us -> none  [per_device(): highest = lax.pmax(best, 'kv')]
    all_gather x1 -> x0, waiting for transfers between devices: 43.7 us -> none  [per_device(): gathered = lax.all_gather(queries, 'kv', axis=2, tiled=True)]
    dot_general x20 -> x0, matrix products: 42.2 us -> none  [the longest x4 30 us: fold_slots(): jnp.einsum('gr,gqhc->rqhc', member_float, factor[..., None] * slot_out, p...]
    gather x8 -> x0, local copies, waits for them, and re-layouts: 25.2 us -> none  [the longest x4 13.1 us: one_block(): cache[pages.reshape(-1)]]
    reduce_scatter x1 -> x0, waiting for transfers between devices: 22.5 us -> none  [per_device(): summed = lax.psum_scatter(scaled, 'kv', scatter_dimension=2, tiled=True)]
    reshape x7 -> x8, local copies, waits for them, and re-layouts: 11.7 us -> 32.8 us  [the longest x2 15.3 us: per_device(): gathered.reshape(count, requests, query_count, local_heads, token_width)]
  transfers between devices with their start and end apart: 2 -> 0, of which waited for: 2 -> 0; matrix products, arithmetic and copies ran while one was open for 3% -> 0% of each run, Pallas kernels for 0% -> 0%
where the time goes in v1:
time: 150 us; the launch traced here: 149 us
  Pallas kernels  90.9 us (61%)
  local copies, waits for them, and re-layouts  51.4 us (34%)
  other arithmetic  6.03 us (4%)
    pallas_call x1, Pallas kernels, gather_queries(): pl.pallas_call(functools.partial(gather_kernel, rows_z), out_shape=jax.Sh...  30.6 us
    pallas_call x1, Pallas kernels, reduce_partials(): pl.pallas_call(functools.partial(reduce_kernel, rows_z), out_shape=jax.Sh...  30.3 us
    pallas_call x1, Pallas kernels, attend(): pl.pallas_call(functools.partial(attend_kernel, latent, query_count), out...  20 us
    reshape x2, local copies, waits for them, and re-layouts, per_device(): gathered.reshape(count, requests, query_count, local_heads, token_width)  15.3 us
    unnamed x7, local copies, waits for them, and re-layouts  12.8 us
    pallas_call x1, Pallas kernels, combine_stats(): pl.pallas_call(functools.partial(stats_kernel, rows_z), out_shape=jax.Sha...  9.94 us
    reshape x1, local copies, waits for them, and re-layouts, per_device(): heads_first.transpose(1, 2, 0, 3, 4).reshape(requests, rows, token_width)  7.18 us
    reshape x1, local copies, waits for them, and re-layouts, per_device(): scaled.astype(jnp.bfloat16)  4.67 us

profile of v1, /device:TPU:0, one launch (start us, length us, event | category | flops | bytes accessed | tf_op | source)
XLA Modules:
  0.0 149.1 jit_solution(12886308107717148012)
XLA Ops:
  0.6 1.4 copy.29.pages
  2.0 1.1 copy.27
  3.1 0.9 reshape.29.x_ref
  3.9 30.6 %gather_queries.1 = bf16[16,48,2304]{2,1,0:T(8,128)(2,1)} custom-call(bf16[48,2304]{1,0:T(8,128)(2,1)} %reshape.29.x_ref), custom_call_target="tpu_custom_call" | custom-call | tf_op jit(solution)/shard_map/gather_queries/pallas_call | solution.py:115
  34.6 9.1 %reshape.30 = bf16[16,16,3,4,576]{4,3,2,1,0:T(4,128)(2,1)} reshape(bf16[16,48,2304]{2,1,0:T(8,128)(2,1)} %gather_queries.1) | data formatting | bytes 7077888 | tf_op jit(solution)/shard_map/reshape | solution.py:394
  43.7 6.2 %copy.41 = bf16[16,16,3,4,576]{4,3,0,2,1:T(4,128)(2,1)} copy(bf16[16,16,3,4,576]{4,3,2,1,0:T(4,128)(2,1)} %reshape.30) | data formatting | bytes 7077888 | tf_op jit(solution)/shard_map/reshape | solution.py:394
  49.8 7.2 %reshape.31.q_ref = bf16[16,192,576]{2,1,0:T(8,128)(2,1)} reshape(bf16[16,3,16,4,576]{4,3,2,1,0:T(4,128)(2,1)} %bitcast.8) | data formatting | bytes 7077888 | tf_op jit(solution)/shard_map/reshape | solution.py:395
  57.0 8.9 %copy.30.cache_ref = bf16[256,16,576]{2,1,0:T(8,128)(2,1)} copy(bf16[256,16,576]{0,2,1:T(8,128)(2,1)} %param.8) | data formatting | bytes 9437184 | tf_op args[1]
  65.9 20.0 %attend.1 = (f32[16,192,512]{2,1,0:T(8,128)}, f32[16,192,128]{2,1,0:T(8,128)}, f32[16,192,128]{2,1,0:T(8,128)}) custom-call(s32[16]{0:T(128)} %counts.1, s32[32]{0:T(128)} %request.1, s32[32]{0:T(128)} %start.1, s32[32]{0:T(128)} %live.1, s32[32,8]{1,0:T(8,128)} %copy.29.pages, bf16[16,192,576]{2,1,0:T(8,128)(2,1)} %reshape.31.q_ref, ...), custom_call_target="tpu_custom_call" | custom-call | tf_op jit(solution)/shard_map/attend/pallas_call | solution.py:189
  85.9 3.1 %slice_reduce_fusion = (f32[16,192]{1,0:T(8,128)S(1)}, f32[16,192]{1,0:T(8,128)S(1)}) fusion(f32[16,192,128]{2,1,0:T(8,128)} %get-tuple-element.7, f32[16,192,128]{2,1,0:T(8,128)} %get-tuple-element.6), kind=kLoop, calls=%fused_computation.3 | loop fusion | bytes 49152 | tf_op jit(solution)/shard_map/slice | solution.py:403
  89.2 0.6 pad_maximum_fusion.in_ref
  89.9 9.9 %combine_stats.1 = f32[2,24,128]{2,1,0:T(8,128)} custom-call(f32[2,24,128]{2,1,0:T(8,128)} %pad_maximum_fusion.in_ref), custom_call_target="tpu_custom_call" | custom-call | tf_op jit(solution)/shard_map/combine_stats/pallas_call | solution.py:258
  99.8 0.7 fusion.1
  100.5 1.4 reshape_squeeze.8
  102.0 0.7 exponential_reduce_fusion
  102.7 4.4 %multiply_convert_fusion = bf16[16,192,512]{2,1,0:T(8,128)(2,1)} fusion(f32[16,192,512]{2,1,0:T(8,128)} %get-tuple-element.5, f32[16,192]{1,0:T(8,128)S(1)} %exponential_reduce_fusion), kind=kLoop, calls=%fused_computation | loop fusion | flops 3145728 | bytes 9449472 | tf_op jit(solution)/shard_map/convert_element_type | solution.py:416
  107.0 4.7 %reshape.32 = bf16[16,3,16,2048]{3,2,1,0:T(8,128)(2,1)S(1)} reshape(bf16[16,192,512]{2,1,0:T(8,128)(2,1)} %multiply_convert_fusion) | data formatting | bytes 6291456 | tf_op jit(solution)/shard_map/reshape | solution.py:416
  111.7 3.4 %copy.32.x_ref = bf16[16,48,2048]{2,1,0:T(8,128)(2,1)} copy(bf16[16,48,2048]{2,0,1:T(8,128)(2,1)S(1)} %bitcast.9) | data formatting | bytes 6291456 | tf_op jit(solution)/shard_map/reshape | solution.py:419
  115.1 30.3 %reduce_partials.1 = f32[48,2048]{1,0:T(8,128)} custom-call(bf16[16,48,2048]{2,1,0:T(8,128)(2,1)} %copy.32.x_ref), custom_call_target="tpu_custom_call" | custom-call | tf_op jit(solution)/shard_map/reduce_partials/pallas_call | solution.py:356
  145.4 1.2 reshape.34
  146.9 0.3 reshape.35
  147.2 0.3 fusion
  147.5 0.8 copy.35
  148.5 0.6 copy.36
  (10 shorter events, 0.5 us)
Async XLA Ops:
  85.9 16.0 %copy-start = (f32[16,192,128]{2,1,0:T(8,128)S(1)}, f32[16,192,128]{2,1,0:T(8,128)}, u32[]{:S(2)}) copy-start(f32[16,192,128]{2,1,0:T(8,128)} %get-tuple-element.6) | copy-start | bytes 4718596

commit v2 on v1

v2 whole, which is shorter than its diff:
```python
import functools

import jax
import jax.numpy as jnp
from jax import lax
from jax.experimental import pallas as pl
from jax.experimental.pallas import tpu as pltpu
from jax.sharding import PartitionSpec as P

ROPE = 64
CORES = 2
LANES = 128
softmax_scale = 192.0 ** (-0.5)
neg_floor = -1e30
slot_group = 4
vmem_limit = 56 * 1024 * 1024


def place(chip_rows):
    index = lax.axis_index("kv")
    z = index // (2 * CORES)
    y = (index // CORES) % 2
    core = index % CORES
    return index, z, y, core


def device_of(z, y, core):
    return (z * 2 + y) * CORES + core


def gather_kernel(
    rows_z, x_ref, picks_ref, cache_ref, o_ref, keys_ref, cache_buf, keys_buf, local_sem, load_sem,
    store_sem, send_sems, recv_sems
):
    page_rows = cache_ref.shape[0]
    slots = keys_ref.shape[0]
    span = picks_ref.shape[0] // slots
    pairs = page_rows // 2
    index, z, y, core = place(rows_z)
    other_y, other_core = 1 - y, 1 - core
    has_up, has_down = z < rows_z - 1, z > 0
    barrier = pltpu.get_barrier_semaphore()

    def greet(target):
        pl.semaphore_signal(barrier, inc=1, device_id={"kv": target})

    pl.when(has_up)(lambda: greet(device_of(z + 1, y, core)))
    pl.when(has_down)(lambda: greet(device_of(z - 1, y, core)))
    greet(device_of(z, other_y, core))
    greet(device_of(z, y, other_core))
    pl.semaphore_wait(barrier, 2 + has_up.astype(jnp.int32) + has_down.astype(jnp.int32))

    def copy(slot, way, source=None):
        target = (
            device_of(jnp.minimum(z + 1, rows_z - 1), y, core),
            device_of(jnp.maximum(z - 1, 0), y, core),
            device_of(z, other_y, core),
            device_of(z, y, other_core),
        )[way]
        return pltpu.make_async_remote_copy(
            src_ref=o_ref.at[slot] if source is None else source,
            dst_ref=o_ref.at[slot],
            send_sem=send_sems.at[slot, way],
            recv_sem=recv_sems.at[slot],
            device_id={"kv": target},
        )

    own = pltpu.make_async_copy(x_ref, o_ref.at[index], local_sem)
    own.start()
    pl.when(has_up)(lambda: copy(index, 0, x_ref).start())
    pl.when(has_down)(lambda: copy(index, 1, x_ref).start())
    copy(index, 2, x_ref).start()
    copy(index, 3, x_ref).start()
    load = pltpu.make_async_copy(cache_ref, cache_buf, load_sem)
    load.start()

    def pick(row):
        chosen = lax.dot_general(
            picks_ref[...], cache_buf[row], (((1,), (1,)), ((), ())),
            preferred_element_type=jnp.float32,
        )
        return chosen.reshape(slots, span, chosen.shape[1])

    def pick_pairs(part):
        for pair in range(pairs * part // rows_z, pairs * (part + 1) // rows_z):
            both = jnp.concatenate([pick(2 * pair), pick(2 * pair + 1)], axis=1)
            first = pair * 2 * span
            keys_buf[:, first : first + 2 * span, :] = both.astype(keys_buf.dtype)

    def from_below(step):
        slot = device_of(z - step, y, core)
        copy(slot, 3).wait_recv()
        pl.when(has_up)(lambda: copy(slot, 0).start())
        copy(slot, 2).start()
        copy(slot, 3).start()

    def from_above(step):
        slot = device_of(z + step, y, core)
        copy(slot, 3).wait_recv()
        pl.when(has_down)(lambda: copy(slot, 1).start())
        copy(slot, 2).start()
        copy(slot, 3).start()

    def across(row):
        slot = device_of(row, other_y, core)
        copy(slot, 3).wait_recv()
        copy(slot, 3).start()

    def across_pair(step):
        if step == 0:
            across(z)
        else:
            pl.when(z >= step)(lambda: across(z - step))
            pl.when(z + step < rows_z)(lambda: across(z + step))

    load.wait()
    pick_pairs(0)
    for step in range(1, rows_z):
        pl.when(z >= step)(functools.partial(from_below, step))
        pl.when(z + step < rows_z)(functools.partial(from_above, step))
        across_pair(step - 1)
        pick_pairs(step)
    store = pltpu.make_async_copy(keys_buf, keys_ref, store_sem)
    store.start()
    across_pair(rows_z - 1)
    for row in range(rows_z):
        for column in range(2):
            copy(device_of(row, column, other_core), 3).wait_recv()

    own.wait()
    store.wait()
    for row in range(rows_z):
        slot = device_of(row, y, core)
        pl.when(has_up & (row <= z))(lambda slot=slot: copy(slot, 0).wait_send())
        pl.when(has_down & (row >= z))(lambda slot=slot: copy(slot, 1).wait_send())
        copy(slot, 2).wait_send()
        copy(slot, 3).wait_send()
        copy(device_of(row, other_y, core), 3).wait_send()


def gather_queries(shard, picks, cache, slots, rows_z):
    count = rows_z * 2 * CORES
    page_rows, token_width, _pages = cache.shape
    keys = jax.ShapeDtypeStruct(
        (slots, picks.shape[0] // slots * page_rows, token_width), cache.dtype
    )
    hbm = pl.BlockSpec(memory_space=pl.ANY)
    return pl.pallas_call(
        functools.partial(gather_kernel, rows_z),
        out_shape=(jax.ShapeDtypeStruct((count,) + shard.shape, shard.dtype), keys),
        in_specs=[hbm, pl.BlockSpec(memory_space=pltpu.VMEM), hbm],
        out_specs=(hbm, hbm),
        scratch_shapes=[
            pltpu.VMEM(cache.shape, cache.dtype),
            pltpu.VMEM(keys.shape, keys.dtype),
            pltpu.SemaphoreType.DMA,
            pltpu.SemaphoreType.DMA,
            pltpu.SemaphoreType.DMA,
            pltpu.SemaphoreType.DMA((count, 4)),
            pltpu.SemaphoreType.DMA((count,)),
        ],
        compiler_params=pltpu.CompilerParams(
            collective_id=0, has_side_effects=True, vmem_limit_bytes=vmem_limit
        ),
        name="gather_queries",
    )(shard, picks, cache)


def attend_whole_kernel(
    latent, query_count, counts, request, start, live, pages, q_ref, cache_ref, numer_ref, best_ref,
    denom_ref
):
    slots, span = pages.shape
    page_rows = cache_ref.shape[1]
    rows = q_ref.shape[1]
    heads = rows // query_count
    keys = span * page_rows
    best_ref[...] = jnp.full(best_ref.shape, neg_floor, jnp.float32)
    denom_ref[...] = jnp.zeros(denom_ref.shape, jnp.float32)
    numer_ref[...] = jnp.zeros(numer_ref.shape, jnp.float32)
    key_ids = lax.broadcasted_iota(jnp.int32, (rows, keys), 1)
    query_ids = lax.broadcasted_iota(jnp.int32, (rows, keys), 0) // heads

    def group(block, carry):
        parts = []
        for offset in range(slot_group):
            slot = block * slot_group + offset
            r = request[slot]
            key_rows = jnp.concatenate([cache_ref[pages[slot, k]] for k in range(span)], axis=0)
            scores = (
                lax.dot_general(
                    q_ref[r], key_rows, (((1,), (1,)), ((), ())),
                    preferred_element_type=jnp.float32,
                )
                * softmax_scale
            )
            bound = (counts[r] - start[slot]) * page_rows - (query_count - 1)
            visible = (key_ids < live[slot] * page_rows) & (key_ids - query_ids < bound)
            top = jnp.max(jnp.where(visible, scores, neg_floor), axis=1, keepdims=True)
            weights = jnp.where(visible, jnp.exp(scores - top), 0.0)
            total = jnp.sum(weights, axis=1, keepdims=True)
            out = jnp.dot(
                weights.astype(jnp.bfloat16), key_rows[:, :latent],
                preferred_element_type=jnp.float32,
            )
            parts.append((r, top, total, out))
        for r, top, total, out in parts:
            old = best_ref[r]
            new = jnp.maximum(old, top)
            kept = jnp.exp(old - new)
            factor = jnp.exp(top - new)
            best_ref[r] = new
            denom_ref[r] = denom_ref[r] * kept + factor * total
            for first in range(0, latent, LANES):
                columns = slice(first, first + LANES)
                numer_ref[r, :, columns] = (
                    numer_ref[r, :, columns] * kept + out[:, columns] * factor
                )
        return carry

    lax.fori_loop(0, slots // slot_group, group, 0)


def attend_whole(queries, cache, counts, request, start, live, pages, latent, query_count):
    requests, rows, _width = queries.shape
    smem = pl.BlockSpec(memory_space=pltpu.SMEM)
    vmem = pl.BlockSpec(memory_space=pltpu.VMEM)
    return pl.pallas_call(
        functools.partial(attend_whole_kernel, latent, query_count),
        out_shape=(
            jax.ShapeDtypeStruct((requests, rows, latent), jnp.float32),
            jax.ShapeDtypeStruct((requests, rows, LANES), jnp.float32),
            jax.ShapeDtypeStruct((requests, rows, LANES), jnp.float32),
        ),
        in_specs=[smem] * 5 + [vmem] * 2,
        out_specs=(vmem, vmem, vmem),
        compiler_params=pltpu.CompilerParams(vmem_limit_bytes=vmem_limit),
        name="attend_whole",
    )(counts, request, start, live, pages, queries, cache)


def attend_blocks_kernel(
    query_count, page_rows, counts, request, start, live, q_ref, keys_ref, part_ref, stats_ref,
    wide_q, narrow_q, numer, best, denom
):
    devices, _rows, shard_width = q_ref.shape
    slots, keys, token_width = keys_ref.shape
    latent = part_ref.shape[2]
    requests, rows = narrow_q.shape[0], narrow_q.shape[1]
    heads = rows // query_count
    local_heads = heads // devices
    span = keys // page_rows
    best[...] = jnp.full(best.shape, neg_floor, jnp.float32)
    denom[...] = jnp.zeros(denom.shape, jnp.float32)
    numer[...] = jnp.zeros(numer.shape, jnp.float32)
    chunks = [(c, min(LANES, token_width - c)) for c in range(0, token_width, LANES)]

    def spread(device, carry):
        for i in range(query_count):
            block = q_ref[device, i * requests : (i + 1) * requests, :].astype(jnp.float32)
            for local in range(local_heads):
                row = i * heads + device * local_heads + local
                for c, (first, size) in enumerate(chunks):
                    at = local * token_width + first
                    wide_q[c, pl.ds(row, requests, stride=rows), 0:size] = block[:, at : at + size]
        return carry

    lax.fori_loop(0, devices, spread, 0)

    def narrow(r, carry):
        for c, (first, size) in enumerate(chunks):
            at = pl.multiple_of(r * rows, 64)
            narrow_q[r, :, first : first + size] = wide_q[c, pl.ds(at, rows), 0:size].astype(
                narrow_q.dtype
            )
        return carry

    lax.fori_loop(0, requests, narrow, 0)

    key_ids = lax.broadcasted_iota(jnp.int32, (rows, keys), 1)
    row_in_page = key_ids // (2 * span) * 2 + key_ids % (2 * span) // span
    key_ids = key_ids % span * page_rows + row_in_page
    query_ids = lax.broadcasted_iota(jnp.int32, (rows, keys), 0) // heads
    reach_ids = key_ids - query_ids

    def group(block, carry):
        parts = []
        for offset in range(slot_group):
            slot = block * slot_group + offset
            r = request[slot]
            key_rows = keys_ref[slot]
            scores = (
                lax.dot_general(
                    narrow_q[r], key_rows, (((1,), (1,)), ((), ())),
                    preferred_element_type=jnp.float32,
                )
                * softmax_scale
            )
            bound = (counts[r] - start[slot]) * page_rows - (query_count - 1)
            visible = (key_ids < live[slot] * page_rows) & (reach_ids < bound)
            top = jnp.max(jnp.where(visible, scores, neg_floor), axis=1, keepdims=True)
            weights = jnp.where(visible, jnp.exp(scores - top), 0.0)
            total = jnp.sum(weights, axis=1, keepdims=True)
            out = jnp.dot(
                weights.astype(jnp.bfloat16), key_rows[:, :latent],
                preferred_element_type=jnp.float32,
            )
            parts.append((r, top, total, out))
        for r, top, total, out in parts:
            at = pl.ds(pl.multiple_of(r * rows, 64), rows)
            old = best[at, :]
            new = jnp.maximum(old, top)
            kept = jnp.exp(old - new)
            factor = jnp.exp(top - new)
            best[at, :] = new
            denom[at, :] = denom[at, :] * kept + factor * total
            for c in range(latent // LANES):
                columns = out[:, c * LANES : (c + 1) * LANES]
                numer[c, at, :] = numer[c, at, :] * kept + columns * factor
        return carry

    lax.fori_loop(0, slots // slot_group, group, 0)

    def hand_out(device, carry):
        tops, totals = [], []
        for local in range(local_heads):
            for i in range(query_count):
                at = pl.ds(i * heads + device * local_heads + local, requests, stride=rows)
                first = (local * query_count + i) * requests
                tops.append(best[at, :])
                totals.append(denom[at, :])
                for c in range(latent // LANES):
                    part_ref[
                        device, first : first + requests, c * LANES : (c + 1) * LANES
                    ] = numer[c, at, :].astype(part_ref.dtype)
        stats_ref[0, pl.ds(device, 1), :] = jnp.concatenate(tops, axis=0).T[0:1, :]
        stats_ref[1, pl.ds(device, 1), :] = jnp.concatenate(totals, axis=0).T[0:1, :]
        return carry

    lax.fori_loop(0, devices, hand_out, 0)


def attend_blocks(queries, keys, counts, request, start, live, query_count, page_rows, latent):
    devices, query_rows, shard_width = queries.shape
    requests = query_rows // query_count
    token_width = keys.shape[2]
    rows = query_count * devices * shard_width // token_width
    block_rows = requests * rows // devices
    smem = pl.BlockSpec(memory_space=pltpu.SMEM)
    vmem = pl.BlockSpec(memory_space=pltpu.VMEM)
    wide = jnp.float32
    return pl.pallas_call(
        functools.partial(attend_blocks_kernel, query_count, page_rows),
        out_shape=(
            jax.ShapeDtypeStruct((devices, block_rows, latent), jnp.bfloat16),
            jax.ShapeDtypeStruct((2, devices, block_rows), wide),
        ),
        in_specs=[smem] * 4 + [vmem] * 2,
        out_specs=(vmem, vmem),
        scratch_shapes=[
            pltpu.VMEM((-(-token_width // LANES), requests * rows, LANES), wide),
            pltpu.VMEM((requests, rows, token_width), queries.dtype),
            pltpu.VMEM((latent // LANES, requests * rows, LANES), wide),
            pltpu.VMEM((requests * rows, LANES), wide),
            pltpu.VMEM((requests * rows, LANES), wide),
        ],
        compiler_params=pltpu.CompilerParams(vmem_limit_bytes=vmem_limit),
        name="attend_blocks",
    )(counts, request, start, live, queries, keys)


def combine(buf, count):
    top = buf[0, 0]
    for item in range(1, count):
        top = jnp.maximum(top, buf[item, 0])
    total = buf[0, 1] * jnp.exp(buf[0, 0] - top)
    for item in range(1, count):
        total = total + buf[item, 1] * jnp.exp(buf[item, 0] - top)
    return top, total


def reduce_kernel(
    rows_z, query_count, x_ref, stats_ref, out_ref, lse_ref, core_in, y_out, y_in, z_out, z_in,
    core_stats, y_stats, z_stats, factors, totals, core_send, core_recv, y_send, y_recv, z_send,
    z_recv, core_sems, y_sems, zs_send, zs_recv
):
    index, z, y, core = place(rows_z)
    other_y, other_core = 1 - y, 1 - core
    partner, across = device_of(z, y, other_core), device_of(z, other_y, core)
    block_rows = x_ref.shape[1]
    barrier = pltpu.get_barrier_semaphore()
    others = [partner, across]
    others += [device_of((z + step) % rows_z, y, core) for step in range(1, rows_z)]
    for target in others:
        pl.semaphore_signal(barrier, inc=1, device_id={"kv": target})
    pl.semaphore_wait(barrier, len(others))

    def row_of(step):
        return (z + step) % rows_z

    steps = list(range(1, rows_z)) + [0]

    def core_copy(side, step):
        column = other_y if side == 0 else y
        return pltpu.make_async_remote_copy(
            src_ref=x_ref.at[device_of(row_of(step), column, other_core)],
            dst_ref=core_in.at[side, step],
            send_sem=core_send.at[side, step],
            recv_sem=core_recv.at[side, step],
            device_id={"kv": partner},
        )

    def y_copy(step):
        return pltpu.make_async_remote_copy(
            src_ref=y_out.at[step], dst_ref=y_in.at[step], send_sem=y_send.at[step],
            recv_sem=y_recv.at[step], device_id={"kv": across},
        )

    def z_copy(step):
        return pltpu.make_async_remote_copy(
            src_ref=z_out.at[step], dst_ref=z_in.at[step], send_sem=z_send.at[step],
            recv_sem=z_recv.at[step],
            device_id={"kv": device_of(row_of(step), y, core)},
        )

    def swap(buf, sems, me, target):
        copy = pltpu.make_async_remote_copy(
            src_ref=buf.at[me], dst_ref=buf.at[me], send_sem=sems.at[0], recv_sem=sems.at[1],
            device_id={"kv": target},
        )
        copy.start()
        return copy

    def stats_copy(step, source):
        return pltpu.make_async_remote_copy(
            src_ref=z_stats.at[source], dst_ref=z_stats.at[source], send_sem=zs_send.at[step],
            recv_sem=zs_recv.at[source], device_id={"kv": device_of(row_of(step), y, core)},
        )

    core_stats[core] = stats_ref[...]
    swapped = swap(core_stats, core_sems, core, partner)
    for side in range(2):
        for step in steps:
            core_copy(side, step).start()
    swapped.wait()
    y_stats[y, 0], y_stats[y, 1] = combine(core_stats, CORES)
    swap(y_stats, y_sems, y, across).wait()
    z_stats[z, 0], z_stats[z, 1] = combine(y_stats, 2)
    for step in range(1, rows_z):
        stats_copy(step, z).start()
    for step in range(1, rows_z):
        stats_copy(step, row_of(step)).wait_recv()
    top, total = combine(z_stats, rows_z)
    lse_ref[...] = top + jnp.log(total)
    totals[...] = total
    for side in range(CORES):
        factors[side] = jnp.exp(core_stats[side, 0] - top)

    def down(row):
        return jnp.broadcast_to(row, (LANES, block_rows)).T

    def scaled(value, side, target):
        spread = down(factors[side, pl.ds(target, 1), :])
        wide = value.astype(jnp.float32)
        return wide * jnp.concatenate([spread] * (wide.shape[1] // LANES), axis=1)

    def both(side, step):
        target = device_of(row_of(step), other_y if side == 0 else y, core)
        core_copy(side, step).wait_recv()
        return scaled(x_ref[target], core, target) + scaled(
            core_in[side, step], other_core, target
        )

    for step in steps:
        y_out[step] = both(0, step).astype(y_out.dtype)
        y_copy(step).start()
    for step in steps:
        total = both(1, step)
        y_copy(step).wait_recv()
        total = total + y_in[step].astype(jnp.float32)
        if step:
            z_out[step] = total.astype(z_out.dtype)
            z_copy(step).start()
    for step in range(1, rows_z):
        z_copy(step).wait_recv()
        total = total + z_in[step].astype(jnp.float32)
    over = down(totals[pl.ds(index, 1), :])
    total = total / jnp.concatenate([over] * (total.shape[1] // LANES), axis=1)
    width = total.shape[1]
    local_rows = out_ref.shape[0]
    for local in range(block_rows // local_rows):
        out_ref[:, local * width : (local + 1) * width] = total[
            local * local_rows : (local + 1) * local_rows
        ].astype(out_ref.dtype)
    for step in range(1, rows_z):
        stats_copy(step, z).wait_send()
    for step in steps:
        core_copy(0, step).wait_send()
        core_copy(1, step).wait_send()
        y_copy(step).wait_send()
        if step:
            z_copy(step).wait_send()


def reduce_partials(parts, stats, rows_z, query_rows, query_count):
    block = parts.shape[1:]
    vmem = pl.BlockSpec(memory_space=pltpu.VMEM)
    dma = pltpu.SemaphoreType.DMA
    width = block[0] // query_rows * block[1]
    return pl.pallas_call(
        functools.partial(reduce_kernel, rows_z, query_count),
        out_shape=(
            jax.ShapeDtypeStruct((query_rows, width), jnp.bfloat16),
            jax.ShapeDtypeStruct(stats.shape[1:], jnp.float32),
        ),
        in_specs=[vmem, vmem],
        out_specs=(vmem, vmem),
        scratch_shapes=[
            pltpu.VMEM((2, rows_z) + block, parts.dtype),
            pltpu.VMEM((rows_z,) + block, parts.dtype),
            pltpu.VMEM((rows_z,) + block, parts.dtype),
            pltpu.VMEM((rows_z,) + block, parts.dtype),
            pltpu.VMEM((rows_z,) + block, parts.dtype),
            pltpu.VMEM((CORES,) + stats.shape, jnp.float32),
            pltpu.VMEM((2,) + stats.shape, jnp.float32),
            pltpu.VMEM((rows_z,) + stats.shape, jnp.float32),
            pltpu.VMEM((CORES,) + stats.shape[1:], jnp.float32),
            pltpu.VMEM(stats.shape[1:], jnp.float32),
            dma((2, rows_z)),
            dma((2, rows_z)),
            dma((rows_z,)),
            dma((rows_z,)),
            dma((rows_z,)),
            dma((rows_z,)),
            dma((2,)),
            dma((2,)),
            dma((rows_z,)),
            dma((rows_z,)),
        ],
        compiler_params=pltpu.CompilerParams(
            collective_id=2, has_side_effects=True, vmem_limit_bytes=vmem_limit
        ),
        name="reduce_partials",
    )(parts, stats)


def per_device(queries, cache, page_counts, slot_request, slot_start, slot_live, slot_pages):
    count = lax.axis_size("kv")
    requests, query_count, shard_width = queries.shape
    page_rows, token_width = cache.shape[1:]
    latent = token_width - ROPE
    heads = count * shard_width // token_width
    rows_z = count // (2 * CORES)
    slots = slot_request.shape[0]
    if shard_width % token_width or rows_z * 2 * CORES != count:
        return per_device_whole(
            queries, cache, page_counts, slot_request, slot_start, slot_live, slot_pages
        )
    local_heads = shard_width // token_width
    query_rows = query_count * requests
    shard = queries.transpose(1, 0, 2).reshape(query_rows, shard_width)
    page_ids = jnp.arange(cache.shape[0], dtype=jnp.int32)
    picks = (slot_pages.reshape(-1, 1) == page_ids[None, :]).astype(cache.dtype)
    gathered, keys = gather_queries(shard, picks, cache.transpose(1, 2, 0), slots, rows_z)
    parts, stats = attend_blocks(
        gathered, keys, page_counts, slot_request, slot_start, slot_live, query_count, page_rows,
        latent,
    )
    attended, lse = reduce_partials(parts, stats, rows_z, query_rows, query_count)
    attended = attended.reshape(query_count, requests, local_heads * latent).transpose(1, 0, 2)
    lse = lse.reshape(count * local_heads, query_count, requests).transpose(2, 1, 0)
    return (attended, lse)


def per_device_whole(queries, cache, page_counts, slot_request, slot_start, slot_live, slot_pages):
    count = lax.axis_size("kv")
    requests, query_count, shard_width = queries.shape
    token_width = cache.shape[2]
    latent = token_width - ROPE
    heads = count * shard_width // token_width
    rows = query_count * heads
    gathered = lax.all_gather(queries, "kv", axis=2, tiled=True)
    query_heads = gathered.reshape(requests, rows, token_width)
    numer, best, denom = attend_whole(
        query_heads, cache, page_counts, slot_request, slot_start, slot_live, slot_pages, latent,
        query_count,
    )
    best, denom = best[:, :, 0], denom[:, :, 0]
    highest = lax.pmax(best, "kv")
    total = lax.psum(denom * jnp.exp(best - highest), "kv")
    scaled = numer * jnp.exp(best - highest)[..., None]
    lse = (highest + jnp.log(total)).reshape(requests, query_count, heads)
    total = total.reshape(requests, query_count, heads)
    flat = lax.optimization_barrier(scaled.reshape(requests * query_count, heads * latent))
    width = heads * latent // count
    summed = lax.psum_scatter(flat, "kv", scatter_dimension=1, tiled=True)
    summed = summed.reshape(requests, query_count, width)
    first_head = lax.axis_index("kv") * width // latent
    picked_heads = max(1, width // latent)
    picked = lax.dynamic_slice_in_dim(total, first_head, picked_heads, 2)
    picked = jnp.repeat(picked, min(width, latent), axis=2)
    return ((summed / picked).astype(jnp.bfloat16), lse)


def solution(mesh):
    in_specs = (
        P("rep", None, "kv"),
        P(("rep", "kv"), None, None),
        P("rep"),
        P(("rep", "kv")),
        P(("rep", "kv")),
        P(("rep", "kv")),
        P(("rep", "kv"), None),
    )
    out_specs = (P("rep", None, "kv"), P("rep", None, None))
    return jax.shard_map(
        per_device, mesh=mesh, in_specs=in_specs, out_specs=out_specs, check_vma=False
    )
```

time: 150 us -> 107 us (0.71)
  local copies, waits for them, and re-layouts: 51.4 us -> 4.02 us
  Pallas kernels: 90.9 us -> 101 us
  other arithmetic: 6.03 us -> 0.77 us
    reshape x8 -> x1, local copies, waits for them, and re-layouts: 32.8 us -> 0.85 us  [per_device(): lse.reshape(count * local_heads, query_count, requests).transpose(2, 1, 0)]
    pallas_call x4 -> x3, Pallas kernels: 90.9 us -> 101 us  [the longest x1 35.8 us: reduce_partials(): pl.pallas_call(functools.partial(reduce_kernel, rows_z, query_count), out...]
    unnamed x7 -> x3, local copies, waits for them, and re-layouts: 12.8 us -> 3.08 us
    convert_element_type x2 -> x1, other arithmetic: 4.71 us -> 0.77 us  [per_device(): picks = (slot_pages.reshape(-1, 1) == page_ids[None, :]).astype(cache.dtype)]
    slice x2 -> x0, local copies, waits for them, and re-layouts: 3.88 us -> none  [the longest x1 3.15 us: per_device(): best, denom = (best[:, :, 0], denom[:, :, 0])]
    another operation x5 -> x0, local copies, waits for them, and re-layouts: 1.71 us -> none  [the longest x2 1.49 us: per_device(): merged[0].reshape(requests, rows)]
where the time goes in v2:
time: 107 us
  Pallas kernels  101 us (94%)
  local copies, waits for them, and re-layouts  4.02 us (4%)
    pallas_call x1, Pallas kernels, reduce_partials(): pl.pallas_call(functools.partial(reduce_kernel, rows_z, query_count), out...  35.8 us
    pallas_call x1, Pallas kernels, attend_blocks(): pl.pallas_call(functools.partial(attend_blocks_kernel, query_count, page_...  34 us
    pallas_call x1, Pallas kernels, gather_queries(): pl.pallas_call(functools.partial(gather_kernel, rows_z), out_shape=(jax.S...  31.5 us
    unnamed x3, local copies, waits for them, and re-layouts  3.08 us

profile of v2, /device:TPU:0, one launch (start us, length us, event | category | flops | bytes accessed | tf_op | source)
XLA Modules:
  0.0 106.8 jit_solution(1937669154055289396)
XLA Ops:
  0.6 0.8 copy.10
  1.4 0.1 eq.15
  1.5 0.8 fusion.picks_ref
  2.2 31.5 %gather_queries.1 = (bf16[16,48,2304]{2,1,0:T(8,128)(2,1)}, bf16[32,128,576]{2,1,0:T(8,128)(2,1)}) custom-call(bf16[48,2304]{1,0:T(8,128)(2,1)} %bitcast.10, bf16[256,256]{1,0:T(8,128)(2,1)} %fusion.picks_ref, bf16[16,576,256]{2,1,0:T(8,128)(2,1)} %bitcast.8), custom_call_target="tpu_custom_call" | custom-call | tf_op jit(solution)/shard_map/gather_queries/pallas_call | solution.py:148
  33.8 34.0 %attend_blocks.1 = (bf16[16,192,512]{2,1,0:T(8,128)(2,1)}, f32[2,16,192]{2,1,0:T(8,128)}) custom-call(s32[16]{0:T(128)} %counts.1, s32[32]{0:T(128)} %request.1, s32[32]{0:T(128)} %start.1, s32[32]{0:T(128)} %live.1, bf16[16,48,2304]{2,1,0:T(8,128)(2,1)} %get-tuple-element.8.q_ref, bf16[32,128,576]{2,1,0:T(8,128)(2,1)} %get-tuple-element.9.keys_ref), custom_call_target="tpu_custom_call" | custom-call | tf_op jit(solution)/shard_map/attend_blocks/pallas_call | solution.py:352
  67.8 35.8 %reduce_partials.1 = (bf16[48,2048]{1,0:T(8,128)(2,1)}, f32[16,192]{1,0:T(8,128)}) custom-call(bf16[16,192,512]{2,1,0:T(8,128)(2,1)} %get-tuple-element.10.x_ref, f32[2,16,192]{2,1,0:T(8,128)} %get-tuple-element.11.stats_ref), custom_call_target="tpu_custom_call" | custom-call | tf_op jit(solution)/shard_map/reduce_partials/pallas_call | solution.py:510
  103.6 0.8 reshape.17
  104.4 0.7 copy.11
  105.1 1.6 %copy.13 = bf16[16,3,2048]{2,0,1:T(8,128)(2,1)} copy(bf16[16,3,2048]{2,0,1:T(8,128)(2,1)} %bitcast.11) | data formatting | bytes 393216

commit v3 on v2

--- a/solution.py
+++ b/solution.py
@@ -29,9 +29,14 @@
 
 
 def gather_kernel(
-    rows_z, x_ref, picks_ref, cache_ref, o_ref, keys_ref, cache_buf, keys_buf, local_sem, load_sem,
-    store_sem, send_sems, recv_sems
+    rows_z, query_count, x_ref, picks_ref, cache_ref, q_ref, keys_ref, o_ref, wide_q, narrow_q,
+    cache_buf, keys_buf, local_sem, load_sem, store_sem, q_sems, send_sems, recv_sems
 ):
+    devices, query_rows, shard_width = o_ref.shape
+    requests, rows, token_width = narrow_q.shape
+    heads = rows // query_count
+    local_heads = heads // devices
+    chunks = [(c, min(LANES, token_width - c)) for c in range(0, token_width, LANES)]
     page_rows = cache_ref.shape[0]
     slots = keys_ref.shape[0]
     span = picks_ref.shape[0] // slots
@@ -113,22 +118,64 @@
             pl.when(z >= step)(lambda: across(z - step))
             pl.when(z + step < rows_z)(lambda: across(z + step))
 
+    def spread(device):
+        def one_query(i, carry):
+            at = pl.ds(pl.multiple_of(i * requests, requests), requests)
+            block = o_ref[device, at, :].astype(jnp.float32)
+            for local in range(local_heads):
+                to = pl.ds(i * heads + device * local_heads + local, requests, stride=rows)
+                for c, (first, size) in enumerate(chunks):
+                    begin = local * token_width + first
+                    wide_q[c, to, 0:size] = block[:, begin : begin + size]
+            return carry
+
+        lax.fori_loop(0, query_count, one_query, 0)
+
+    def arrange(column, step):
+        def pair(row):
+            spread(device_of(row, column, core))
+            copy(device_of(row, column, other_core), 3).wait_recv()
+            spread(device_of(row, column, other_core))
+
+        if step == 0:
+            pair(z)
+        else:
+            pl.when(z >= step)(lambda: pair(z - step))
+            pl.when(z + step < rows_z)(lambda: pair(z + step))
+
     load.wait()
     pick_pairs(0)
+    own.wait()
     for step in range(1, rows_z):
         pl.when(z >= step)(functools.partial(from_below, step))
         pl.when(z + step < rows_z)(functools.partial(from_above, step))
         across_pair(step - 1)
         pick_pairs(step)
+        arrange(y, step - 1)
+        if step > 1:
+            arrange(other_y, step - 2)
     store = pltpu.make_async_copy(keys_buf, keys_ref, store_sem)
     store.start()
     across_pair(rows_z - 1)
-    for row in range(rows_z):
-        for column in range(2):
-            copy(device_of(row, column, other_core), 3).wait_recv()
-
-    own.wait()
+    arrange(y, rows_z - 1)
+    if rows_z > 1:
+        arrange(other_y, rows_z - 2)
+    arrange(other_y, rows_z - 1)
+
+    def hand_on(r):
+        return pltpu.make_async_copy(narrow_q.at[r], q_ref.at[r], q_sems.at[r])
+
+    def narrow(r, carry):
+        at = pl.ds(pl.multiple_of(r * rows, 64), rows)
+        for c, (first, size) in enumerate(chunks):
+            narrow_q[r, :, first : first + size] = wide_q[c, at, 0:size].astype(narrow_q.dtype)
+        hand_on(r).start()
+        return carry
+
+    lax.fori_loop(0, requests, narrow, 0)
     store.wait()
+    for r in range(requests):
+        hand_on(r).wait()
     for row in range(rows_z):
         slot = device_of(row, y, core)
         pl.when(has_up & (row <= z))(lambda slot=slot: copy(slot, 0).wait_send())
@@ -138,24 +185,31 @@
         copy(device_of(row, other_y, core), 3).wait_send()
 
 
-def gather_queries(shard, picks, cache, slots, rows_z):
+def gather_queries(shard, picks, cache, slots, rows_z, query_count):
     count = rows_z * 2 * CORES
     page_rows, token_width, _pages = cache.shape
+    requests = shard.shape[0] // query_count
+    rows = query_count * count * shard.shape[1] // token_width
     keys = jax.ShapeDtypeStruct(
         (slots, picks.shape[0] // slots * page_rows, token_width), cache.dtype
     )
+    grouped = jax.ShapeDtypeStruct((requests, rows, token_width), shard.dtype)
     hbm = pl.BlockSpec(memory_space=pl.ANY)
     return pl.pallas_call(
-        functools.partial(gather_kernel, rows_z),
-        out_shape=(jax.ShapeDtypeStruct((count,) + shard.shape, shard.dtype), keys),
+        functools.partial(gather_kernel, rows_z, query_count),
+        out_shape=(grouped, keys),
         in_specs=[hbm, pl.BlockSpec(memory_space=pltpu.VMEM), hbm],
         out_specs=(hbm, hbm),
         scratch_shapes=[
+            pltpu.VMEM((count,) + shard.shape, shard.dtype),
+            pltpu.VMEM((-(-token_width // LANES), requests * rows, LANES), jnp.float32),
+            pltpu.VMEM(grouped.shape, grouped.dtype),
             pltpu.VMEM(cache.shape, cache.dtype),
             pltpu.VMEM(keys.shape, keys.dtype),
             pltpu.SemaphoreType.DMA,
             pltpu.SemaphoreType.DMA,
             pltpu.SemaphoreType.DMA,
+            pltpu.SemaphoreType.DMA((requests,)),
             pltpu.SemaphoreType.DMA((count, 4)),
             pltpu.SemaphoreType.DMA((count,)),
         ],
@@ -240,12 +294,26 @@
 
 
 def attend_blocks_kernel(
-    query_count, page_rows, counts, request, start, live, q_ref, keys_ref, part_ref, stats_ref,
-    wide_q, narrow_q, numer, best, denom
+    query_count, page_rows, counts, request, start, live, q_hbm, keys_hbm, part_hbm, stats_ref,
+    narrow_q, keys_ref, part_ref, numer, best, denom, q_sem, key_sems, part_sems
 ):
-    devices, _rows, shard_width = q_ref.shape
+    devices = part_ref.shape[0]
     slots, keys, token_width = keys_ref.shape
     latent = part_ref.shape[2]
+    queries_in = pltpu.make_async_copy(q_hbm, narrow_q, q_sem)
+    queries_in.start()
+
+    def keys_in(block):
+        at = pl.ds(block * slot_group, slot_group)
+        return pltpu.make_async_copy(keys_hbm.at[at], keys_ref.at[at], key_sems.at[block])
+
+    def part_out(device):
+        return pltpu.make_async_copy(
+            part_ref.at[device], part_hbm.at[device], part_sems.at[device]
+        )
+
+    for block in range(slots // slot_group):
+        keys_in(block).start()
     requests, rows = narrow_q.shape[0], narrow_q.shape[1]
     heads = rows // query_count
     local_heads = heads // devices
@@ -253,38 +321,16 @@
     best[...] = jnp.full(best.shape, neg_floor, jnp.float32)
     denom[...] = jnp.zeros(denom.shape, jnp.float32)
     numer[...] = jnp.zeros(numer.shape, jnp.float32)
-    chunks = [(c, min(LANES, token_width - c)) for c in range(0, token_width, LANES)]
-
-    def spread(device, carry):
-        for i in range(query_count):
-            block = q_ref[device, i * requests : (i + 1) * requests, :].astype(jnp.float32)
-            for local in range(local_heads):
-                row = i * heads + device * local_heads + local
-                for c, (first, size) in enumerate(chunks):
-                    at = local * token_width + first
-                    wide_q[c, pl.ds(row, requests, stride=rows), 0:size] = block[:, at : at + size]
-        return carry
-
-    lax.fori_loop(0, devices, spread, 0)
-
-    def narrow(r, carry):
-        for c, (first, size) in enumerate(chunks):
-            at = pl.multiple_of(r * rows, 64)
-            narrow_q[r, :, first : first + size] = wide_q[c, pl.ds(at, rows), 0:size].astype(
-                narrow_q.dtype
-            )
-        return carry
-
-    lax.fori_loop(0, requests, narrow, 0)
-
     key_ids = lax.broadcasted_iota(jnp.int32, (rows, keys), 1)
     row_in_page = key_ids // (2 * span) * 2 + key_ids % (2 * span) // span
     key_ids = key_ids % span * page_rows + row_in_page
     query_ids = lax.broadcasted_iota(jnp.int32, (rows, keys), 0) // heads
     reach_ids = key_ids - query_ids
+    queries_in.wait()
 
     def group(block, carry):
         parts = []
+        keys_in(block).wait()
         for offset in range(slot_group):
             slot = block * slot_group + offset
             r = request[slot]
@@ -334,20 +380,24 @@
                         device, first : first + requests, c * LANES : (c + 1) * LANES
                     ] = numer[c, at, :].astype(part_ref.dtype)
         stats_ref[0, pl.ds(device, 1), :] = jnp.concatenate(tops, axis=0).T[0:1, :]
+        part_out(device).start()
         stats_ref[1, pl.ds(device, 1), :] = jnp.concatenate(totals, axis=0).T[0:1, :]
         return carry
 
     lax.fori_loop(0, devices, hand_out, 0)
-
-
-def attend_blocks(queries, keys, counts, request, start, live, query_count, page_rows, latent):
-    devices, query_rows, shard_width = queries.shape
-    requests = query_rows // query_count
-    token_width = keys.shape[2]
-    rows = query_count * devices * shard_width // token_width
+    for device in range(devices):
+        part_out(device).wait()
+
+
+def attend_blocks(
+    queries, keys, counts, request, start, live, devices, query_count, page_rows, latent
+):
+    requests, rows, token_width = queries.shape
     block_rows = requests * rows // devices
     smem = pl.BlockSpec(memory_space=pltpu.SMEM)
     vmem = pl.BlockSpec(memory_space=pltpu.VMEM)
+    hbm = pl.BlockSpec(memory_space=pl.ANY)
+    dma = pltpu.SemaphoreType.DMA
     wide = jnp.float32
     return pl.pallas_call(
         functools.partial(attend_blocks_kernel, query_count, page_rows),
@@ -355,14 +405,18 @@
             jax.ShapeDtypeStruct((devices, block_rows, latent), jnp.bfloat16),
             jax.ShapeDtypeStruct((2, devices, block_rows), wide),
         ),
-        in_specs=[smem] * 4 + [vmem] * 2,
-        out_specs=(vmem, vmem),
+        in_specs=[smem] * 4 + [hbm] * 2,
+        out_specs=(hbm, vmem),
         scratch_shapes=[
-            pltpu.VMEM((-(-token_width // LANES), requests * rows, LANES), wide),
-            pltpu.VMEM((requests, rows, token_width), queries.dtype),
+            pltpu.VMEM(queries.shape, queries.dtype),
+            pltpu.VMEM(keys.shape, keys.dtype),
+            pltpu.VMEM((devices, block_rows, latent), jnp.bfloat16),
             pltpu.VMEM((latent // LANES, requests * rows, LANES), wide),
             pltpu.VMEM((requests * rows, LANES), wide),
             pltpu.VMEM((requests * rows, LANES), wide),
+            dma,
+            dma((keys.shape[0] // slot_group,)),
+            dma((devices,)),
         ],
         compiler_params=pltpu.CompilerParams(vmem_limit_bytes=vmem_limit),
         name="attend_blocks",
@@ -380,14 +434,14 @@
 
 
 def reduce_kernel(
-    rows_z, query_count, x_ref, stats_ref, out_ref, lse_ref, core_in, y_out, y_in, z_out, z_in,
+    rows_z, x_hbm, stats_ref, out_ref, lse_ref, x_ref, x_sems, core_in, y_out, y_in, z_out, z_in,
     core_stats, y_stats, z_stats, factors, totals, core_send, core_recv, y_send, y_recv, z_send,
     z_recv, core_sems, y_sems, zs_send, zs_recv
 ):
     index, z, y, core = place(rows_z)
     other_y, other_core = 1 - y, 1 - core
     partner, across = device_of(z, y, other_core), device_of(z, other_y, core)
-    block_rows = x_ref.shape[1]
+    block_rows = x_ref.shape[2]
     barrier = pltpu.get_barrier_semaphore()
     others = [partner, across]
     others += [device_of((z + step) % rows_z, y, core) for step in range(1, rows_z)]
@@ -403,7 +457,7 @@
     def core_copy(side, step):
         column = other_y if side == 0 else y
         return pltpu.make_async_remote_copy(
-            src_ref=x_ref.at[device_of(row_of(step), column, other_core)],
+            src_ref=x_hbm.at[device_of(row_of(step), column, other_core)],
             dst_ref=core_in.at[side, step],
             send_sem=core_send.at[side, step],
             recv_sem=core_recv.at[side, step],
@@ -437,11 +491,21 @@
             recv_sem=zs_recv.at[source], device_id={"kv": device_of(row_of(step), y, core)},
         )
 
+    def x_copy(side, step):
+        column = other_y if side == 0 else y
+        return pltpu.make_async_copy(
+            x_hbm.at[device_of(row_of(step), column, core)], x_ref.at[side, step],
+            x_sems.at[side, step],
+        )
+
     core_stats[core] = stats_ref[...]
     swapped = swap(core_stats, core_sems, core, partner)
     for side in range(2):
         for step in steps:
             core_copy(side, step).start()
+    for side in range(2):
+        for step in steps:
+            x_copy(side, step).start()
     swapped.wait()
     y_stats[y, 0], y_stats[y, 1] = combine(core_stats, CORES)
     swap(y_stats, y_sems, y, across).wait()
@@ -466,8 +530,9 @@
 
     def both(side, step):
         target = device_of(row_of(step), other_y if side == 0 else y, core)
+        x_copy(side, step).wait()
         core_copy(side, step).wait_recv()
-        return scaled(x_ref[target], core, target) + scaled(
+        return scaled(x_ref[side, step], core, target) + scaled(
             core_in[side, step], other_core, target
         )
 
@@ -502,20 +567,22 @@
             z_copy(step).wait_send()
 
 
-def reduce_partials(parts, stats, rows_z, query_rows, query_count):
+def reduce_partials(parts, stats, rows_z, query_rows):
     block = parts.shape[1:]
     vmem = pl.BlockSpec(memory_space=pltpu.VMEM)
     dma = pltpu.SemaphoreType.DMA
     width = block[0] // query_rows * block[1]
     return pl.pallas_call(
-        functools.partial(reduce_kernel, rows_z, query_count),
+        functools.partial(reduce_kernel, rows_z),
         out_shape=(
             jax.ShapeDtypeStruct((query_rows, width), jnp.bfloat16),
             jax.ShapeDtypeStruct(stats.shape[1:], jnp.float32),
         ),
-        in_specs=[vmem, vmem],
+        in_specs=[pl.BlockSpec(memory_space=pl.ANY), vmem],
         out_specs=(vmem, vmem),
         scratch_shapes=[
+            pltpu.VMEM((2, rows_z) + block, parts.dtype),
+            dma((2, rows_z)),
             pltpu.VMEM((2, rows_z) + block, parts.dtype),
             pltpu.VMEM((rows_z,) + block, parts.dtype),
             pltpu.VMEM((rows_z,) + block, parts.dtype),
@@ -561,12 +628,14 @@
     shard = queries.transpose(1, 0, 2).reshape(query_rows, shard_width)
     page_ids = jnp.arange(cache.shape[0], dtype=jnp.int32)
     picks = (slot_pages.reshape(-1, 1) == page_ids[None, :]).astype(cache.dtype)
-    gathered, keys = gather_queries(shard, picks, cache.transpose(1, 2, 0), slots, rows_z)
+    gathered, keys = gather_queries(
+        shard, picks, cache.transpose(1, 2, 0), slots, rows_z, query_count
+    )
     parts, stats = attend_blocks(
-        gathered, keys, page_counts, slot_request, slot_start, slot_live, query_count, page_rows,
-        latent,
+        gathered, keys, page_counts, slot_request, slot_start, slot_live, count, query_count,
+        page_rows, latent,
     )
-    attended, lse = reduce_partials(parts, stats, rows_z, query_rows, query_count)
+    attended, lse = reduce_partials(parts, stats, rows_z, query_rows)
     attended = attended.reshape(query_count, requests, local_heads * latent).transpose(1, 0, 2)
     lse = lse.reshape(count * local_heads, query_count, requests).transpose(2, 1, 0)
     return (attended, lse)

time: 107 us -> 99.6 us (0.931)
  Pallas kernels: 101 us -> 93.5 us
    pallas_call x1, Pallas kernels: 34 us -> 25.5 us  [attend_blocks(): pl.pallas_call(functools.partial(attend_blocks_kernel, query_count, page_...]
where the time goes in v3:
time: 99.6 us; the launch traced here: 99 us
  Pallas kernels  93.5 us (94%)
  local copies, waits for them, and re-layouts  4.02 us (4%)
    pallas_call x1, Pallas kernels, gather_queries(): pl.pallas_call(functools.partial(gather_kernel, rows_z, query_count), out...  34.1 us
    pallas_call x1, Pallas kernels, reduce_partials(): pl.pallas_call(functools.partial(reduce_kernel, rows_z), out_shape=(jax.S...  33.9 us
    pallas_call x1, Pallas kernels, attend_blocks(): pl.pallas_call(functools.partial(attend_blocks_kernel, query_count, page_...  25.5 us
    unnamed x3, local copies, waits for them, and re-layouts  3.08 us

profile of v3, /device:TPU:0, one launch (start us, length us, event | category | flops | bytes accessed | tf_op | source)
XLA Modules:
  0.0 99.0 jit_solution(6807540540768922650)
XLA Ops:
  0.6 0.8 copy.10
  1.4 0.1 eq.15
  1.5 0.8 fusion.picks_ref
  2.2 34.1 %gather_queries.1 = (bf16[16,192,576]{2,1,0:T(8,128)(2,1)}, bf16[32,128,576]{2,1,0:T(8,128)(2,1)}) custom-call(bf16[48,2304]{1,0:T(8,128)(2,1)} %bitcast.10, bf16[256,256]{1,0:T(8,128)(2,1)} %fusion.picks_ref, bf16[16,576,256]{2,1,0:T(8,128)(2,1)} %bitcast.8), custom_call_target="tpu_custom_call" | custom-call | tf_op jit(solution)/shard_map/gather_queries/pallas_call | solution.py:198
  36.3 25.5 %attend_blocks.1 = (bf16[16,192,512]{2,1,0:T(8,128)(2,1)}, f32[2,16,192]{2,1,0:T(8,128)}) custom-call(s32[16]{0:T(128)} %counts.1, s32[32]{0:T(128)} %request.1, s32[32]{0:T(128)} %start.1, s32[32]{0:T(128)} %live.1, bf16[16,192,576]{2,1,0:T(8,128)(2,1)} %get-tuple-element.8.q_hbm, bf16[32,128,576]{2,1,0:T(8,128)(2,1)} %get-tuple-element.9.keys_hbm), custom_call_target="tpu_custom_call" | custom-call | tf_op jit(solution)/shard_map/attend_blocks/pallas_call | solution.py:402
  61.9 33.9 %reduce_partials.1 = (bf16[48,2048]{1,0:T(8,128)(2,1)}, f32[16,192]{1,0:T(8,128)}) custom-call(bf16[16,192,512]{2,1,0:T(8,128)(2,1)} %get-tuple-element.10.x_hbm, f32[2,16,192]{2,1,0:T(8,128)} %get-tuple-element.11.stats_ref), custom_call_target="tpu_custom_call" | custom-call | tf_op jit(solution)/shard_map/reduce_partials/pallas_call | solution.py:575
  95.8 0.8 reshape.17
  96.6 0.7 copy.11
  97.3 1.6 %copy.13 = bf16[16,3,2048]{2,0,1:T(8,128)(2,1)} copy(bf16[16,3,2048]{2,0,1:T(8,128)(2,1)} %bitcast.11) | data formatting | bytes 393216

commit v4 on v3

--- a/solution.py
+++ b/solution.py
@@ -12,7 +12,7 @@
 LANES = 128
 softmax_scale = 192.0 ** (-0.5)
 neg_floor = -1e30
-slot_group = 4
+slot_group = 8
 vmem_limit = 56 * 1024 * 1024
 
 
@@ -435,7 +435,7 @@
 
 def reduce_kernel(
     rows_z, x_hbm, stats_ref, out_ref, lse_ref, x_ref, x_sems, core_in, y_out, y_in, z_out, z_in,
-    core_stats, y_stats, z_stats, factors, totals, core_send, core_recv, y_send, y_recv, z_send,
+    core_stats, y_stats, z_stats, near, factors, totals, core_send, core_recv, y_send, y_recv, z_send,
     z_recv, core_sems, y_sems, zs_send, zs_recv
 ):
     index, z, y, core = place(rows_z)
@@ -507,11 +507,36 @@
         for step in steps:
             x_copy(side, step).start()
     swapped.wait()
-    y_stats[y, 0], y_stats[y, 1] = combine(core_stats, CORES)
-    swap(y_stats, y_sems, y, across).wait()
-    z_stats[z, 0], z_stats[z, 1] = combine(y_stats, 2)
-    for step in range(1, rows_z):
-        stats_copy(step, z).start()
+    chip_top, chip_total = combine(core_stats, CORES)
+    y_stats[y, 0], y_stats[y, 1] = chip_top, chip_total
+    across_stats = swap(y_stats, y_sems, y, across)
+    for side in range(CORES):
+        near[side] = jnp.exp(core_stats[side, 0] - chip_top)
+
+    def down(row):
+        return jnp.broadcast_to(row, (LANES, block_rows)).T
+
+    def scaled(value, scale, target):
+        spread = down(scale[pl.ds(target, 1), :])
+        wide = value.astype(jnp.float32)
+        return wide * jnp.concatenate([spread] * (wide.shape[1] // LANES), axis=1)
+
+    def both(scales, side, step):
+        target = device_of(row_of(step), other_y if side == 0 else y, core)
+        x_copy(side, step).wait()
+        core_copy(side, step).wait_recv()
+        return scaled(x_ref[side, step], scales.at[core], target) + scaled(
+            core_in[side, step], scales.at[other_core], target
+        )
+
+    for order, step in enumerate(steps):
+        y_out[step] = both(near, 0, step).astype(y_out.dtype)
+        y_copy(step).start()
+        if order == 0:
+            across_stats.wait()
+            z_stats[z, 0], z_stats[z, 1] = combine(y_stats, 2)
+            for other in range(1, rows_z):
+                stats_copy(other, z).start()
     for step in range(1, rows_z):
         stats_copy(step, row_of(step)).wait_recv()
     top, total = combine(z_stats, rows_z)
@@ -519,30 +544,13 @@
     totals[...] = total
     for side in range(CORES):
         factors[side] = jnp.exp(core_stats[side, 0] - top)
-
-    def down(row):
-        return jnp.broadcast_to(row, (LANES, block_rows)).T
-
-    def scaled(value, side, target):
-        spread = down(factors[side, pl.ds(target, 1), :])
-        wide = value.astype(jnp.float32)
-        return wide * jnp.concatenate([spread] * (wide.shape[1] // LANES), axis=1)
-
-    def both(side, step):
-        target = device_of(row_of(step), other_y if side == 0 else y, core)
-        x_copy(side, step).wait()
-        core_copy(side, step).wait_recv()
-        return scaled(x_ref[side, step], core, target) + scaled(
-            core_in[side, step], other_core, target
-        )
-
+    factors[CORES] = jnp.exp(y_stats[other_y, 0] - top)
     for step in steps:
-        y_out[step] = both(0, step).astype(y_out.dtype)
-        y_copy(step).start()
-    for step in steps:
-        total = both(1, step)
+        total = both(factors, 1, step)
         y_copy(step).wait_recv()
-        total = total + y_in[step].astype(jnp.float32)
+        total = total + scaled(
+            y_in[step], factors.at[CORES], device_of(row_of(step), y, core)
+        )
         if step:
             z_out[step] = total.astype(z_out.dtype)
             z_copy(step).start()
@@ -592,6 +600,7 @@
             pltpu.VMEM((2,) + stats.shape, jnp.float32),
             pltpu.VMEM((rows_z,) + stats.shape, jnp.float32),
             pltpu.VMEM((CORES,) + stats.shape[1:], jnp.float32),
+            pltpu.VMEM((CORES + 1,) + stats.shape[1:], jnp.float32),
             pltpu.VMEM(stats.shape[1:], jnp.float32),
             dma((2, rows_z)),
             dma((2, rows_z)),

time: 99.6 us -> 94.5 us (0.949)
  Pallas kernels: 93.5 us -> 88.7 us
    pallas_call x1, Pallas kernels: 33.9 us -> 30.1 us  [reduce_partials(): pl.pallas_call(functools.partial(reduce_kernel, rows_z), out_shape=(jax.S...]
    pallas_call x1, Pallas kernels: 25.5 us -> 24.5 us  [attend_blocks(): pl.pallas_call(functools.partial(attend_blocks_kernel, query_count, page_...]
where the time goes in v4:
time: 94.5 us; the launch traced here: 94.1 us
  Pallas kernels  88.7 us (94%)
  local copies, waits for them, and re-layouts  4.02 us (4%)
    pallas_call x1, Pallas kernels, gather_queries(): pl.pallas_call(functools.partial(gather_kernel, rows_z, query_count), out...  34.1 us
    pallas_call x1, Pallas kernels, reduce_partials(): pl.pallas_call(functools.partial(reduce_kernel, rows_z), out_shape=(jax.S...  30.1 us
    pallas_call x1, Pallas kernels, attend_blocks(): pl.pallas_call(functools.partial(attend_blocks_kernel, query_count, page_...  24.5 us
    unnamed x3, local copies, waits for them, and re-layouts  3.08 us

profile of v4, /device:TPU:0, one launch (start us, length us, event | category | flops | bytes accessed | tf_op | source)
XLA Modules:
  0.0 94.1 jit_solution(7160659306878976942)
XLA Ops:
  0.6 0.8 copy.10
  1.4 0.1 eq.15
  1.5 0.8 fusion.picks_ref
  2.2 34.1 %gather_queries.1 = (bf16[16,192,576]{2,1,0:T(8,128)(2,1)}, bf16[32,128,576]{2,1,0:T(8,128)(2,1)}) custom-call(bf16[48,2304]{1,0:T(8,128)(2,1)} %bitcast.10, bf16[256,256]{1,0:T(8,128)(2,1)} %fusion.picks_ref, bf16[16,576,256]{2,1,0:T(8,128)(2,1)} %bitcast.8), custom_call_target="tpu_custom_call" | custom-call | tf_op jit(solution)/shard_map/gather_queries/pallas_call | solution.py:198
  36.3 24.5 %attend_blocks.1 = (bf16[16,192,512]{2,1,0:T(8,128)(2,1)}, f32[2,16,192]{2,1,0:T(8,128)}) custom-call(s32[16]{0:T(128)} %counts.1, s32[32]{0:T(128)} %request.1, s32[32]{0:T(128)} %start.1, s32[32]{0:T(128)} %live.1, bf16[16,192,576]{2,1,0:T(8,128)(2,1)} %get-tuple-element.8.q_hbm, bf16[32,128,576]{2,1,0:T(8,128)(2,1)} %get-tuple-element.9.keys_hbm), custom_call_target="tpu_custom_call" | custom-call | tf_op jit(solution)/shard_map/attend_blocks/pallas_call | solution.py:402
  60.9 30.1 %reduce_partials.1 = (bf16[48,2048]{1,0:T(8,128)(2,1)}, f32[16,192]{1,0:T(8,128)}) custom-call(bf16[16,192,512]{2,1,0:T(8,128)(2,1)} %get-tuple-element.10.x_hbm, f32[2,16,192]{2,1,0:T(8,128)} %get-tuple-element.11.stats_ref), custom_call_target="tpu_custom_call" | custom-call | tf_op jit(solution)/shard_map/reduce_partials/pallas_call | solution.py:583
  91.0 0.8 reshape.17
  91.8 0.7 copy.11
  92.5 1.6 %copy.13 = bf16[16,3,2048]{2,0,1:T(8,128)(2,1)} copy(bf16[16,3,2048]{2,0,1:T(8,128)(2,1)} %bitcast.11) | data formatting | bytes 393216
